TPU v7x, 16 devices: a whole 2x2x2 slice. The times are simulated.
16 devices in a mesh: tp: 4 (over z, y), pp: 4 (over x, core).
Axes of the slice: x: 2, y: 2, z: 2, core: 2. Of those that a mesh axis runs over, the one named last changes fastest.
Arguments:
- x_micro: bfloat16 [6, 1, 1536, 2560], replicated
- ln1_gain: bfloat16 [4, 2560], P('pp')
- ln1_bias: bfloat16 [4, 2560], P('pp')
- w_qkv: bfloat16 [4, 2560, 32, 240], P('pp', None, 'tp')
- b_qkv: bfloat16 [4, 32, 240], P('pp', 'tp')
- w_dense: bfloat16 [4, 32, 80, 2560], P('pp', 'tp')
- b_dense: bfloat16 [4, 2560], P('pp')
- ln2_gain: bfloat16 [4, 2560], P('pp')
- ln2_bias: bfloat16 [4, 2560], P('pp')
- w_up: bfloat16 [4, 2560, 10240], P('pp', None, 'tp')
- b_up: bfloat16 [4, 10240], P('pp', 'tp')
- w_down: bfloat16 [4, 10240, 2560], P('pp', 'tp')
- b_down: bfloat16 [4, 2560], P('pp')
Outputs:
- output: bfloat16 [6, 1, 1536, 2560], replicated
All inputs are finite; a program needn't handle non-finite values.
Results may differ from a plain program's by a relative error of at most 0.0185461.
Values are sent between devices in bfloat16 or wider.
A program may use at most 1 GiB of HBM per device.

v0:
```python
import jax
import jax.numpy as jnp
from jax import lax
from jax.sharding import PartitionSpec as P


def layer_norm(x_act, gain, bias):
    x_f32 = x_act.astype(jnp.float32)
    centered = x_f32 - jnp.mean(x_f32, axis=-1, keepdims=True)
    spread = jnp.mean(centered * centered, axis=-1, keepdims=True)
    normed = centered * lax.rsqrt(spread + 1e-5)
    return (normed * gain.astype(jnp.float32) + bias.astype(jnp.float32)).astype(jnp.bfloat16)


def rotary_tables(seq_len, rot_dims):
    inv_freq = 1.0 / (10000.0 ** (jnp.arange(0, rot_dims, 2).astype(jnp.float32) / rot_dims))
    angles = jnp.arange(seq_len).astype(jnp.float32)[:, None] * inv_freq[None, :]
    angles = jnp.concatenate([angles, angles], axis=-1)
    return jnp.cos(angles), jnp.sin(angles)


def apply_rotary(heads_in, cos_tab, sin_tab, rot_dims):
    half_rot = rot_dims // 2
    rot_part = heads_in[..., :rot_dims].astype(jnp.float32)
    rotated = jnp.concatenate([-rot_part[..., half_rot:], rot_part[..., :half_rot]], axis=-1)
    mixed = rot_part * cos_tab[:, None, :] + rotated * sin_tab[:, None, :]
    return jnp.concatenate([mixed.astype(jnp.bfloat16), heads_in[..., rot_dims:]], axis=-1)


def branch_sum(x_act, weights, cos_tab, sin_tab):
    ln1_gain, ln1_bias, w_qkv, b_qkv, w_dense, ln2_gain, ln2_bias, w_up, b_up, w_down = weights
    head_dim = w_dense.shape[1]
    rot_dims = head_dim // 4
    positions = jnp.arange(x_act.shape[1])
    ln_attn = layer_norm(x_act, ln1_gain, ln1_bias)
    qkv_proj = jnp.einsum("bsd,dhe->bshe", ln_attn, w_qkv, preferred_element_type=jnp.float32)
    qkv_proj = (qkv_proj + b_qkv.astype(jnp.float32)).astype(jnp.bfloat16)
    query = apply_rotary(qkv_proj[..., :head_dim], cos_tab, sin_tab, rot_dims)
    key_rot = apply_rotary(qkv_proj[..., head_dim:2 * head_dim], cos_tab, sin_tab, rot_dims)
    values = qkv_proj[..., 2 * head_dim:]
    scores = jnp.einsum("bqhd,bkhd->bhqk", query, key_rot, preferred_element_type=jnp.float32) * head_dim ** -0.5
    causal = positions[:, None] >= positions[None, :]
    probs = jax.nn.softmax(jnp.where(causal, scores, -1e30), axis=-1).astype(jnp.bfloat16)
    context = jnp.einsum("bhqk,bkhd->bqhd", probs, values, preferred_element_type=jnp.float32).astype(jnp.bfloat16)
    attn_part = jnp.einsum("bqhd,hde->bqe", context, w_dense, preferred_element_type=jnp.float32)
    ln_mlp = layer_norm(x_act, ln2_gain, ln2_bias)
    hidden = jnp.einsum("bsd,df->bsf", ln_mlp, w_up, preferred_element_type=jnp.float32) + b_up.astype(jnp.float32)
    hidden = jax.nn.gelu(hidden, approximate=False).astype(jnp.bfloat16)
    mlp_part = jnp.einsum("bsf,fd->bsd", hidden, w_down, preferred_element_type=jnp.float32)
    return attn_part + mlp_part


def solution(mesh):
    n_stages = mesh.shape["pp"]
    in_specs = (P(), P("pp", None), P("pp", None), P("pp", None, "tp", None), P("pp", "tp", None),
                P("pp", "tp", None, None), P("pp", None), P("pp", None), P("pp", None),
                P("pp", None, "tp"), P("pp", "tp"), P("pp", "tp", None), P("pp", None))

    def device_fn(x_micro, ln1_gain, ln1_bias, w_qkv, b_qkv, w_dense, b_dense, ln2_gain, ln2_bias, w_up, b_up, w_down, b_down):
        weights = (ln1_gain[0], ln1_bias[0], w_qkv[0], b_qkv[0], w_dense[0],
                   ln2_gain[0], ln2_bias[0], w_up[0], b_up[0], w_down[0])
        bias_sum = b_dense[0].astype(jnp.float32) + b_down[0].astype(jnp.float32)
        n_micro = x_micro.shape[0]
        cos_tab, sin_tab = rotary_tables(x_micro.shape[2], w_dense.shape[2] // 4)
        stage = lax.axis_index("pp")
        is_last = stage == n_stages - 1
        forward_pairs = [(source, source + 1) for source in range(n_stages - 1)]

        def run_layer(x_act):
            return branch_sum(x_act, weights, cos_tab, sin_tab).astype(jnp.bfloat16)

        def tick(step, carry):
            incoming, result = carry
            micro_id = step - stage
            valid = jnp.logical_and(micro_id >= 0, micro_id < n_micro)
            slot = jnp.clip(micro_id, 0, n_micro - 1)
            first_in = lax.dynamic_index_in_dim(x_micro, slot, 0, keepdims=False)
            x_act = jnp.where(stage == 0, first_in, incoming)
            tp_part = lax.cond(valid, run_layer, jnp.zeros_like, x_act)
            summed = lax.psum(tp_part, "tp")
            out_act = (x_act.astype(jnp.float32) + bias_sum + summed.astype(jnp.float32)).astype(jnp.bfloat16)
            current = lax.dynamic_index_in_dim(result, slot, 0, keepdims=False)
            keep = jnp.logical_and(valid, is_last)
            result = lax.dynamic_update_index_in_dim(result, jnp.where(keep, out_act, current), slot, 0)
            incoming = lax.ppermute(out_act, "pp", forward_pairs)
            return incoming, result

        start = (jnp.zeros(x_micro.shape[1:], jnp.bfloat16), jnp.zeros_like(x_micro))
        _, result = lax.fori_loop(0, n_micro + n_stages - 1, tick, start)
        return lax.psum(result, "pp")

    return jax.shard_map(device_fn, mesh=mesh, in_specs=in_specs, out_specs=P(), check_vma=False)
```

profile of v0, /device:TPU:0, one launch (start us, length us, event | category | flops | bytes accessed | tf_op | source)
XLA Modules:
  0.0 5004.8 jit_solution(16662182913775669233)
XLA Ops:
  16.0 15.2 broadcast_in_dim.20
  34.8 4080.0 %while.16 = (s32[]{:T(128)}, bf16[1,1536,2560]{2,1,0:T(8,128)(2,1)}, bf16[6,1,1536,2560]{3,2,1,0:T(8,128)(2,1)}, pred[]{:T(512)}, s32[]{:T(128)}, /*index=5*/bf1...) while((s32[]{:T(128)}, ...), condition=%wide.region_8.9_spmd, body=%wide.region_0.8_spmd.sunk | while | flops 66941448192 | bytes 593183168 | solution.py:89
  42.2 201.2 %conditional.2 = (bf16[1,1536,2560]{2,1,0:T(8,128)(2,1)}) conditional(s32[]{:T(128)} %convert_element_type.213, () %tuple.52, (bf16[1,1536,2560]{2,1,0:T(8,128)(2,1)}, bf16[2560]{0:T(1024)(128)(2,1)}, bf16[2560]{0:T(1024)(128)(2,1)}, bf16[2560,8,240]{0,2,1:T(8,128)(2,1)}, bf16[8,240]{1,0:T(8,128)(2,1)}, /*index=5*/f32[1536,20]{0,1:T(8,128)S(1)}, ...), branch_computations={%region_1.1_spmd, %region_2.6_spmd} | conditional | flops 66909990912 | bytes 433878976 | solution.py:79
  53.6 21.0 fusion.32
  86.4 38.7 fusion.58
  125.0 32.2 fusion.59
  157.3 60.8 %fusion.17 = bf16[1536,2560]{1,0:T(8,128)(2,1)} fusion(bf16[2560,2560]{1,0:T(8,128)(2,1)} %get-tuple-element.412, bf16[1,1536,2560]{2,1,0:T(8,128)(2,1)} %get-tuple-element.402, f32[2560]{0:T(1024)S(1)} %convert_element_type.113, f32[2560]{0:T(1024)S(1)} %convert_element_type.111, f32[2560]{0:T(1024)S(1)} %convert_element_type.110, ...), kind=kOutput, calls=%fused_computation.23 | convolution fusion | flops 20415774720 | bytes 28878848 | tf_op jit(solution)/shard_map/while/body/eval_jaxpr/cond/branch_1_fun/bsd,df->bsf/dot_general | solution.py:47
  218.2 25.0 fusion.26
  250.3 151.1 %all-reduce.5.cloned.1.call-done = bf16[1,1536,2560]{2,1,0:T(8,128)(2,1)} async-done(((bf16[1,1536,2560]{2,1,0:T(8,128)(2,1)}), bf16[1,1536,2560]{2,1,0:T(8,128)(2,1)}) %all-reduce.5.cloned.1.call-update) | async-done | bytes 7864336 | tf_op jit(solution)/shard_map/while/body/eval_jaxpr/psum | solution.py:80
  401.5 13.9 bitcast_dynamic-update-slice_fusion.2
  436.7 201.2 %conditional.2 = (bf16[1,1536,2560]{2,1,0:T(8,128)(2,1)}) conditional(s32[]{:T(128)} %convert_element_type.213, () %tuple.52, (bf16[1,1536,2560]{2,1,0:T(8,128)(2,1)}, bf16[2560]{0:T(1024)(128)(2,1)}, bf16[2560]{0:T(1024)(128)(2,1)}, bf16[2560,8,240]{0,2,1:T(8,128)(2,1)}, bf16[8,240]{1,0:T(8,128)(2,1)}, /*index=5*/f32[1536,20]{0,1:T(8,128)S(1)}, ...), branch_computations={%region_1.1_spmd, %region_2.6_spmd} | conditional | flops 66909990912 | bytes 433878976 | solution.py:79
  448.1 21.0 fusion.32
  480.9 38.4 fusion.58
  519.3 32.2 fusion.59
  551.6 60.8 %fusion.17 = bf16[1536,2560]{1,0:T(8,128)(2,1)} fusion(bf16[2560,2560]{1,0:T(8,128)(2,1)} %get-tuple-element.412, bf16[1,1536,2560]{2,1,0:T(8,128)(2,1)} %get-tuple-element.402, f32[2560]{0:T(1024)S(1)} %convert_element_type.113, f32[2560]{0:T(1024)S(1)} %convert_element_type.111, f32[2560]{0:T(1024)S(1)} %convert_element_type.110, ...), kind=kOutput, calls=%fused_computation.23 | convolution fusion | flops 20415774720 | bytes 28878848 | tf_op jit(solution)/shard_map/while/body/eval_jaxpr/cond/branch_1_fun/bsd,df->bsf/dot_general | solution.py:47
  612.5 25.0 fusion.26
  644.9 224.5 %all-reduce.5.cloned.1.call-done = bf16[1,1536,2560]{2,1,0:T(8,128)(2,1)} async-done(((bf16[1,1536,2560]{2,1,0:T(8,128)(2,1)}), bf16[1,1536,2560]{2,1,0:T(8,128)(2,1)}) %all-reduce.5.cloned.1.call-update) | async-done | bytes 7864336 | tf_op jit(solution)/shard_map/while/body/eval_jaxpr/psum | solution.py:80
  869.4 13.9 bitcast_dynamic-update-slice_fusion.2
  904.3 201.2 %conditional.2 = (bf16[1,1536,2560]{2,1,0:T(8,128)(2,1)}) conditional(s32[]{:T(128)} %convert_element_type.213, () %tuple.52, (bf16[1,1536,2560]{2,1,0:T(8,128)(2,1)}, bf16[2560]{0:T(1024)(128)(2,1)}, bf16[2560]{0:T(1024)(128)(2,1)}, bf16[2560,8,240]{0,2,1:T(8,128)(2,1)}, bf16[8,240]{1,0:T(8,128)(2,1)}, /*index=5*/f32[1536,20]{0,1:T(8,128)S(1)}, ...), branch_computations={%region_1.1_spmd, %region_2.6_spmd} | conditional | flops 66909990912 | bytes 433878976 | solution.py:79
  915.7 21.1 fusion.32
  948.5 38.7 fusion.58
  987.2 32.2 fusion.59
  1019.5 60.8 %fusion.17 = bf16[1536,2560]{1,0:T(8,128)(2,1)} fusion(bf16[2560,2560]{1,0:T(8,128)(2,1)} %get-tuple-element.412, bf16[1,1536,2560]{2,1,0:T(8,128)(2,1)} %get-tuple-element.402, f32[2560]{0:T(1024)S(1)} %convert_element_type.113, f32[2560]{0:T(1024)S(1)} %convert_element_type.111, f32[2560]{0:T(1024)S(1)} %convert_element_type.110, ...), kind=kOutput, calls=%fused_computation.23 | convolution fusion | flops 20415774720 | bytes 28878848 | tf_op jit(solution)/shard_map/while/body/eval_jaxpr/cond/branch_1_fun/bsd,df->bsf/dot_general | solution.py:47
  1080.3 25.0 fusion.26
  1112.5 226.9 %all-reduce.5.cloned.1.call-done = bf16[1,1536,2560]{2,1,0:T(8,128)(2,1)} async-done(((bf16[1,1536,2560]{2,1,0:T(8,128)(2,1)}), bf16[1,1536,2560]{2,1,0:T(8,128)(2,1)}) %all-reduce.5.cloned.1.call-update) | async-done | bytes 7864336 | tf_op jit(solution)/shard_map/while/body/eval_jaxpr/psum | solution.py:80
  1339.4 13.9 bitcast_dynamic-update-slice_fusion.2
  1357.8 8.9 collective-permute-done
  1374.6 201.2 %conditional.2 = (bf16[1,1536,2560]{2,1,0:T(8,128)(2,1)}) conditional(s32[]{:T(128)} %convert_element_type.213, () %tuple.52, (bf16[1,1536,2560]{2,1,0:T(8,128)(2,1)}, bf16[2560]{0:T(1024)(128)(2,1)}, bf16[2560]{0:T(1024)(128)(2,1)}, bf16[2560,8,240]{0,2,1:T(8,128)(2,1)}, bf16[8,240]{1,0:T(8,128)(2,1)}, /*index=5*/f32[1536,20]{0,1:T(8,128)S(1)}, ...), branch_computations={%region_1.1_spmd, %region_2.6_spmd} | conditional | flops 66909990912 | bytes 433878976 | solution.py:79
  1386.1 21.0 fusion.32
  1418.8 38.4 fusion.58
  1457.2 32.2 fusion.59
  1489.6 60.8 %fusion.17 = bf16[1536,2560]{1,0:T(8,128)(2,1)} fusion(bf16[2560,2560]{1,0:T(8,128)(2,1)} %get-tuple-element.412, bf16[1,1536,2560]{2,1,0:T(8,128)(2,1)} %get-tuple-element.402, f32[2560]{0:T(1024)S(1)} %convert_element_type.113, f32[2560]{0:T(1024)S(1)} %convert_element_type.111, f32[2560]{0:T(1024)S(1)} %convert_element_type.110, ...), kind=kOutput, calls=%fused_computation.23 | convolution fusion | flops 20415774720 | bytes 28878848 | tf_op jit(solution)/shard_map/while/body/eval_jaxpr/cond/branch_1_fun/bsd,df->bsf/dot_general | solution.py:47
  1550.4 25.0 fusion.26
  1582.8 227.1 %all-reduce.5.cloned.1.call-done = bf16[1,1536,2560]{2,1,0:T(8,128)(2,1)} async-done(((bf16[1,1536,2560]{2,1,0:T(8,128)(2,1)}), bf16[1,1536,2560]{2,1,0:T(8,128)(2,1)}) %all-reduce.5.cloned.1.call-update) | async-done | bytes 7864336 | tf_op jit(solution)/shard_map/while/body/eval_jaxpr/psum | solution.py:80
  1809.9 13.9 bitcast_dynamic-update-slice_fusion.2
  1844.8 201.2 %conditional.2 = (bf16[1,1536,2560]{2,1,0:T(8,128)(2,1)}) conditional(s32[]{:T(128)} %convert_element_type.213, () %tuple.52, (bf16[1,1536,2560]{2,1,0:T(8,128)(2,1)}, bf16[2560]{0:T(1024)(128)(2,1)}, bf16[2560]{0:T(1024)(128)(2,1)}, bf16[2560,8,240]{0,2,1:T(8,128)(2,1)}, bf16[8,240]{1,0:T(8,128)(2,1)}, /*index=5*/f32[1536,20]{0,1:T(8,128)S(1)}, ...), branch_computations={%region_1.1_spmd, %region_2.6_spmd} | conditional | flops 66909990912 | bytes 433878976 | solution.py:79
  1856.3 21.0 fusion.32
  1889.0 38.6 fusion.58
  1927.7 32.2 fusion.59
  1960.0 60.8 %fusion.17 = bf16[1536,2560]{1,0:T(8,128)(2,1)} fusion(bf16[2560,2560]{1,0:T(8,128)(2,1)} %get-tuple-element.412, bf16[1,1536,2560]{2,1,0:T(8,128)(2,1)} %get-tuple-element.402, f32[2560]{0:T(1024)S(1)} %convert_element_type.113, f32[2560]{0:T(1024)S(1)} %convert_element_type.111, f32[2560]{0:T(1024)S(1)} %convert_element_type.110, ...), kind=kOutput, calls=%fused_computation.23 | convolution fusion | flops 20415774720 | bytes 28878848 | tf_op jit(solution)/shard_map/while/body/eval_jaxpr/cond/branch_1_fun/bsd,df->bsf/dot_general | solution.py:47
  2020.8 25.0 fusion.26
  2053.0 227.1 %all-reduce.5.cloned.1.call-done = bf16[1,1536,2560]{2,1,0:T(8,128)(2,1)} async-done(((bf16[1,1536,2560]{2,1,0:T(8,128)(2,1)}), bf16[1,1536,2560]{2,1,0:T(8,128)(2,1)}) %all-reduce.5.cloned.1.call-update) | async-done | bytes 7864336 | tf_op jit(solution)/shard_map/while/body/eval_jaxpr/psum | solution.py:80
  2280.1 13.9 bitcast_dynamic-update-slice_fusion.2
  2298.5 8.9 collective-permute-done
  2315.3 201.2 %conditional.2 = (bf16[1,1536,2560]{2,1,0:T(8,128)(2,1)}) conditional(s32[]{:T(128)} %convert_element_type.213, () %tuple.52, (bf16[1,1536,2560]{2,1,0:T(8,128)(2,1)}, bf16[2560]{0:T(1024)(128)(2,1)}, bf16[2560]{0:T(1024)(128)(2,1)}, bf16[2560,8,240]{0,2,1:T(8,128)(2,1)}, bf16[8,240]{1,0:T(8,128)(2,1)}, /*index=5*/f32[1536,20]{0,1:T(8,128)S(1)}, ...), branch_computations={%region_1.1_spmd, %region_2.6_spmd} | conditional | flops 66909990912 | bytes 433878976 | solution.py:79
  2326.7 21.0 fusion.32
  2359.5 38.4 fusion.58
  2397.9 32.2 fusion.59
  2430.2 60.8 %fusion.17 = bf16[1536,2560]{1,0:T(8,128)(2,1)} fusion(bf16[2560,2560]{1,0:T(8,128)(2,1)} %get-tuple-element.412, bf16[1,1536,2560]{2,1,0:T(8,128)(2,1)} %get-tuple-element.402, f32[2560]{0:T(1024)S(1)} %convert_element_type.113, f32[2560]{0:T(1024)S(1)} %convert_element_type.111, f32[2560]{0:T(1024)S(1)} %convert_element_type.110, ...), kind=kOutput, calls=%fused_computation.23 | convolution fusion | flops 20415774720 | bytes 28878848 | tf_op jit(solution)/shard_map/while/body/eval_jaxpr/cond/branch_1_fun/bsd,df->bsf/dot_general | solution.py:47
  2491.1 25.0 fusion.26
  2523.4 227.1 %all-reduce.5.cloned.1.call-done = bf16[1,1536,2560]{2,1,0:T(8,128)(2,1)} async-done(((bf16[1,1536,2560]{2,1,0:T(8,128)(2,1)}), bf16[1,1536,2560]{2,1,0:T(8,128)(2,1)}) %all-reduce.5.cloned.1.call-update) | async-done | bytes 7864336 | tf_op jit(solution)/shard_map/while/body/eval_jaxpr/psum | solution.py:80
  2750.6 13.9 bitcast_dynamic-update-slice_fusion.2
  2785.5 9.8 conditional.2
  2802.2 418.6 %all-reduce.5.cloned.1.call-done = bf16[1,1536,2560]{2,1,0:T(8,128)(2,1)} async-done(((bf16[1,1536,2560]{2,1,0:T(8,128)(2,1)}), bf16[1,1536,2560]{2,1,0:T(8,128)(2,1)}) %all-reduce.5.cloned.1.call-update) | async-done | bytes 7864336 | tf_op jit(solution)/shard_map/while/body/eval_jaxpr/psum | solution.py:80
  3220.8 13.9 bitcast_dynamic-update-slice_fusion.2
  3255.5 9.8 conditional.2
  3272.3 419.0 %all-reduce.5.cloned.1.call-done = bf16[1,1536,2560]{2,1,0:T(8,128)(2,1)} async-done(((bf16[1,1536,2560]{2,1,0:T(8,128)(2,1)}), bf16[1,1536,2560]{2,1,0:T(8,128)(2,1)}) %all-reduce.5.cloned.1.call-update) | async-done | bytes 7864336 | tf_op jit(solution)/shard_map/while/body/eval_jaxpr/psum | solution.py:80
  3691.3 13.9 bitcast_dynamic-update-slice_fusion.2
  3709.7 8.9 collective-permute-done
  3726.0 9.8 conditional.2
  3742.8 343.5 %all-reduce.5.cloned.1.call-done = bf16[1,1536,2560]{2,1,0:T(8,128)(2,1)} async-done(((bf16[1,1536,2560]{2,1,0:T(8,128)(2,1)}), bf16[1,1536,2560]{2,1,0:T(8,128)(2,1)}) %all-reduce.5.cloned.1.call-update) | async-done | bytes 7864336 | tf_op jit(solution)/shard_map/while/body/eval_jaxpr/psum | solution.py:80
  4086.2 13.9 bitcast_dynamic-update-slice_fusion.2
  4115.3 851.1 %all-reduce.3.cloned.1.call-done = bf16[6,1,1536,2560]{3,2,1,0:T(8,128)(2,1)} async-done(((bf16[6,1,1536,2560]{3,2,1,0:T(8,128)(2,1)}), bf16[6,1,1536,2560]{3,2,1,0:T(8,128)(2,1)}) %all-reduce.3.cloned.1.call-update) | async-done | bytes 47185936 | tf_op jit(solution)/shard_map/psum | solution.py:90
  4966.4 31.0 copy.30
  (343 shorter events, 385.5 us)
Async XLA Ops:
  34.8 366.7 %all-reduce.5.cloned.1.call-start = ((), (), s32[]{:S(2)}) async-start(), calls=%async_computation.1 | async-start | bytes 15728640 | tf_op jit(solution)/shard_map/while/body/eval_jaxpr/psum | solution.py:80
  125.0 32.3 copy-start.8
  125.0 32.3 copy-start.6
  125.0 32.3 copy-start.7
  157.3 60.8 %copy-start.9 = (bf16[2560,2560]{1,0:T(8,128)(2,1)S(1)}, bf16[2560,2560]{1,0:T(8,128)(2,1)}, u32[]{:S(2)}) copy-start(bf16[2560,2560]{1,0:T(8,128)(2,1)} %get-tuple-element.414) | copy-start | bytes 39321604 | tf_op jit(solution)/shard_map/while/body/eval_jaxpr/cond
  243.4 158.1 %copy-start.5 = (f32[2560]{0:T(1024)S(1)}, f32[2560]{0:T(1024)}, u32[]{:S(2)}) copy-start(f32[2560]{0:T(1024)} %get-tuple-element.675) | copy-start | bytes 30724 | tf_op jit(solution)/shard_map/while
  401.5 27.4 copy-start.2
  401.5 27.4 copy-start.4
  415.3 13.5 collective-permute-start
  429.3 440.0 %all-reduce.5.cloned.1.call-start = ((), (), s32[]{:S(2)}) async-start(), calls=%async_computation.1 | async-start | bytes 15728640 | tf_op jit(solution)/shard_map/while/body/eval_jaxpr/psum | solution.py:80
  519.3 32.3 copy-start.8
  519.3 32.3 copy-start.6
  519.3 32.3 copy-start.7
  551.6 60.9 %copy-start.9 = (bf16[2560,2560]{1,0:T(8,128)(2,1)S(1)}, bf16[2560,2560]{1,0:T(8,128)(2,1)}, u32[]{:S(2)}) copy-start(bf16[2560,2560]{1,0:T(8,128)(2,1)} %get-tuple-element.414) | copy-start | bytes 39321604 | tf_op jit(solution)/shard_map/while/body/eval_jaxpr/cond
  637.9 231.5 %copy-start.5 = (f32[2560]{0:T(1024)S(1)}, f32[2560]{0:T(1024)}, u32[]{:S(2)}) copy-start(f32[2560]{0:T(1024)} %get-tuple-element.675) | copy-start | bytes 30724 | tf_op jit(solution)/shard_map/while
  869.4 27.4 copy-start.2
  869.4 27.4 copy-start.4
  883.2 13.5 collective-permute-start
  896.9 442.5 %all-reduce.5.cloned.1.call-start = ((), (), s32[]{:S(2)}) async-start(), calls=%async_computation.1 | async-start | bytes 15728640 | tf_op jit(solution)/shard_map/while/body/eval_jaxpr/psum | solution.py:80
  987.1 32.3 copy-start.8
  987.2 32.3 copy-start.6
  987.2 32.3 copy-start.7
  1019.5 60.8 %copy-start.9 = (bf16[2560,2560]{1,0:T(8,128)(2,1)S(1)}, bf16[2560,2560]{1,0:T(8,128)(2,1)}, u32[]{:S(2)}) copy-start(bf16[2560,2560]{1,0:T(8,128)(2,1)} %get-tuple-element.414) | copy-start | bytes 39321604 | tf_op jit(solution)/shard_map/while/body/eval_jaxpr/cond
  1105.5 233.9 %copy-start.5 = (f32[2560]{0:T(1024)S(1)}, f32[2560]{0:T(1024)}, u32[]{:S(2)}) copy-start(f32[2560]{0:T(1024)} %get-tuple-element.675) | copy-start | bytes 30724 | tf_op jit(solution)/shard_map/while
  1339.4 27.4 copy-start.4
  1353.3 13.5 collective-permute-start
  1367.2 442.6 %all-reduce.5.cloned.1.call-start = ((), (), s32[]{:S(2)}) async-start(), calls=%async_computation.1 | async-start | bytes 15728640 | tf_op jit(solution)/shard_map/while/body/eval_jaxpr/psum | solution.py:80
  1457.2 32.3 copy-start.8
  1457.2 32.3 copy-start.6
  1457.2 32.3 copy-start.7
  1489.5 60.9 %copy-start.9 = (bf16[2560,2560]{1,0:T(8,128)(2,1)S(1)}, bf16[2560,2560]{1,0:T(8,128)(2,1)}, u32[]{:S(2)}) copy-start(bf16[2560,2560]{1,0:T(8,128)(2,1)} %get-tuple-element.414) | copy-start | bytes 39321604 | tf_op jit(solution)/shard_map/while/body/eval_jaxpr/cond
  1575.8 234.1 %copy-start.5 = (f32[2560]{0:T(1024)S(1)}, f32[2560]{0:T(1024)}, u32[]{:S(2)}) copy-start(f32[2560]{0:T(1024)} %get-tuple-element.675) | copy-start | bytes 30724 | tf_op jit(solution)/shard_map/while
  1809.9 27.4 copy-start.2
  1809.9 27.4 copy-start.4
  1823.7 13.5 collective-permute-start
  1837.4 442.6 %all-reduce.5.cloned.1.call-start = ((), (), s32[]{:S(2)}) async-start(), calls=%async_computation.1 | async-start | bytes 15728640 | tf_op jit(solution)/shard_map/while/body/eval_jaxpr/psum | solution.py:80
  1927.7 32.3 copy-start.8
  1927.7 32.3 copy-start.6
  1927.7 32.3 copy-start.7
  1960.0 60.8 %copy-start.9 = (bf16[2560,2560]{1,0:T(8,128)(2,1)S(1)}, bf16[2560,2560]{1,0:T(8,128)(2,1)}, u32[]{:S(2)}) copy-start(bf16[2560,2560]{1,0:T(8,128)(2,1)} %get-tuple-element.414) | copy-start | bytes 39321604 | tf_op jit(solution)/shard_map/while/body/eval_jaxpr/cond
  2046.0 234.1 %copy-start.5 = (f32[2560]{0:T(1024)S(1)}, f32[2560]{0:T(1024)}, u32[]{:S(2)}) copy-start(f32[2560]{0:T(1024)} %get-tuple-element.675) | copy-start | bytes 30724 | tf_op jit(solution)/shard_map/while
  2280.1 27.4 copy-start.4
  2293.9 13.5 collective-permute-start
  2307.9 442.6 %all-reduce.5.cloned.1.call-start = ((), (), s32[]{:S(2)}) async-start(), calls=%async_computation.1 | async-start | bytes 15728640 | tf_op jit(solution)/shard_map/while/body/eval_jaxpr/psum | solution.py:80
  2397.9 32.3 copy-start.8
  2397.9 32.3 copy-start.6
  2397.9 32.3 copy-start.7
  2430.2 60.9 %copy-start.9 = (bf16[2560,2560]{1,0:T(8,128)(2,1)S(1)}, bf16[2560,2560]{1,0:T(8,128)(2,1)}, u32[]{:S(2)}) copy-start(bf16[2560,2560]{1,0:T(8,128)(2,1)} %get-tuple-element.414) | copy-start | bytes 39321604 | tf_op jit(solution)/shard_map/while/body/eval_jaxpr/cond
  2516.5 234.1 %copy-start.5 = (f32[2560]{0:T(1024)S(1)}, f32[2560]{0:T(1024)}, u32[]{:S(2)}) copy-start(f32[2560]{0:T(1024)} %get-tuple-element.675) | copy-start | bytes 30724 | tf_op jit(solution)/shard_map/while
  2750.6 27.4 copy-start.4
  2764.4 13.5 collective-permute-start
  2778.1 442.7 %all-reduce.5.cloned.1.call-start = ((), (), s32[]{:S(2)}) async-start(), calls=%async_computation.1 | async-start | bytes 15728640 | tf_op jit(solution)/shard_map/while/body/eval_jaxpr/psum | solution.py:80
  2795.3 425.5 %copy-start.5 = (f32[2560]{0:T(1024)S(1)}, f32[2560]{0:T(1024)}, u32[]{:S(2)}) copy-start(f32[2560]{0:T(1024)} %get-tuple-element.675) | copy-start | bytes 30724 | tf_op jit(solution)/shard_map/while
  3220.8 27.4 copy-start.4
  3234.6 13.5 collective-permute-start
  3248.2 443.1 %all-reduce.5.cloned.1.call-start = ((), (), s32[]{:S(2)}) async-start(), calls=%async_computation.1 | async-start | bytes 15728640 | tf_op jit(solution)/shard_map/while/body/eval_jaxpr/psum | solution.py:80
  3265.3 425.9 %copy-start.5 = (f32[2560]{0:T(1024)S(1)}, f32[2560]{0:T(1024)}, u32[]{:S(2)}) copy-start(f32[2560]{0:T(1024)} %get-tuple-element.675) | copy-start | bytes 30724 | tf_op jit(solution)/shard_map/while
  3691.3 27.4 copy-start.4
  3705.1 13.5 collective-permute-start
  3718.6 367.6 %all-reduce.5.cloned.1.call-start = ((), (), s32[]{:S(2)}) async-start(), calls=%async_computation.1 | async-start | bytes 15728640 | tf_op jit(solution)/shard_map/while/body/eval_jaxpr/psum | solution.py:80
  3735.8 350.4 %copy-start.5 = (f32[2560]{0:T(1024)S(1)}, f32[2560]{0:T(1024)}, u32[]{:S(2)}) copy-start(f32[2560]{0:T(1024)} %get-tuple-element.675) | copy-start | bytes 30724 | tf_op jit(solution)/shard_map/while
  4086.2 27.4 copy-start.4
  4100.1 13.5 collective-permute-start
  4114.7 851.7 %all-reduce.3.cloned.1.call-start = ((), (), s32[]{:S(2)}) async-start(), calls=%async_computation | async-start | bytes 94371840 | tf_op jit(solution)/shard_map/psum | solution.py:90
  (42 other events, 422.4 us)
Sparse Core Ops, SparseCore 0:
  243.6 157.8 all-reduce.4
  638.1 231.2 all-reduce.4
  1105.7 233.6 all-reduce.4
  1576.0 233.8 all-reduce.4
  2046.2 233.8 all-reduce.4
  2516.7 233.8 all-reduce.4
  2795.4 425.3 all-reduce.4
  3265.5 425.7 all-reduce.4
  3736.0 350.1 all-reduce.4
Sparse Core Ops, SparseCore 1:
  4117.7 848.6 all-reduce.2
where the time goes:
time: 5010 us; the launch traced here: 5000 us
  waiting for transfers between devices  3400 us (68%)
  matrix products  1070 us (21%)
  other arithmetic  313 us (6%)
  local copies, waits for them, and re-layouts  148 us (3%)
    psum x9, waiting for transfers between devices, tick(): summed = lax.psum(tp_part, 'tp')  2460 us
    psum x1, waiting for transfers between devices, device_fn(): return lax.psum(result, 'pp')  851 us
    dot_general x6, matrix products, branch_sum(): jnp.einsum('bsd,df->bsf', ln_mlp, w_up, preferred_element_type=jnp.float32)  365 us
    sub x6, matrix products, branch_sum(): jax.nn.softmax(jnp.where(causal, scores, -1e+30), axis=-1)  231 us
    dot_general x6, matrix products, branch_sum(): jnp.einsum('bqhd,hde->bqe', context, w_dense, preferred_element_type=jnp....  193 us
    dot_general x6, matrix products, branch_sum(): jnp.einsum('bsf,fd->bsd', hidden, w_down, preferred_element_type=jnp.floa...  150 us
    cond x6, matrix products  126 us
    dynamic_update_slice x9, other arithmetic, tick(): lax.dynamic_update_index_in_dim(result, jnp.where(keep, out_act, current)...  125 us
  transfers between devices with their start and end apart: 19, of which 19 were waited for; matrix products, arithmetic and copies ran while one was open for 1% of the time, Pallas kernels for 0%

commit v1 on v0

v1 whole, which is shorter than its diff:
```python
import functools

import jax
import jax.numpy as jnp
from jax import lax
from jax.experimental import pallas as pl
from jax.experimental.pallas import tpu as pltpu
from jax.sharding import PartitionSpec as P

CHUNKS = 2
Q_BLOCK = 256
ROT_PAD = 32
LOG2E = 1.4426950408889634


def ln_kernel(stage_ref, first_ref, later_ref, gain1_ref, bias1_ref, gain2_ref, bias2_ref, attn_ref, mlp_ref):
    group = 16

    def run(source):
        def body(index, _):
            span = pl.ds(pl.multiple_of(index * group, group), group)
            x_f32 = source[span, :].astype(jnp.float32)
            centered = x_f32 - jnp.mean(x_f32, axis=-1, keepdims=True)
            spread = jnp.mean(centered * centered, axis=-1, keepdims=True)
            normed = centered * lax.rsqrt(spread + 1e-5)
            attn_ref[span, :] = (normed * gain1_ref[...] + bias1_ref[...]).astype(jnp.bfloat16)
            mlp_ref[span, :] = (normed * gain2_ref[...] + bias2_ref[...]).astype(jnp.bfloat16)
            return 0

        lax.fori_loop(0, attn_ref.shape[0] // group, body, 0, unroll=2)

    @pl.when(stage_ref[0] == 0)
    def _():
        run(first_ref.at[0])

    @pl.when(stage_ref[0] != 0)
    def _():
        run(later_ref)


def layer_norms(stage, slot, first, later, gain1, bias1, gain2, bias2):
    rows, width = later.shape
    block = 128
    scalars = jnp.stack([stage, slot]).astype(jnp.int32)
    vec = pl.BlockSpec((1, width), lambda j, s: (0, 0))
    return pl.pallas_call(
        ln_kernel,
        out_shape=[jax.ShapeDtypeStruct((rows, width), jnp.bfloat16)] * 2,
        grid_spec=pltpu.PrefetchScalarGridSpec(
            num_scalar_prefetch=1,
            grid=(rows // block,),
            in_specs=[
                pl.BlockSpec((1, block, width), lambda j, s: (s[1], jnp.where(s[0] == 0, j, 0), 0)),
                pl.BlockSpec((block, width), lambda j, s: (jnp.where(s[0] == 0, 0, j), 0)),
                vec, vec, vec, vec,
            ],
            out_specs=[pl.BlockSpec((block, width), lambda j, s: (j, 0))] * 2,
        ),
        cost_estimate=pl.CostEstimate(flops=rows * width * 600, bytes_accessed=rows * width * 6, transcendentals=0),
        name="layer_norms",
    )(scalars, first, later, gain1, bias1, gain2, bias2)


def rotate(x_t, swap, cos_t, sin_t):
    top = swap.shape[0]
    swapped = jnp.dot(swap, x_t, preferred_element_type=jnp.float32)
    mixed = x_t[:top].astype(jnp.float32) * cos_t + swapped * sin_t
    return jnp.concatenate([mixed, x_t[top:].astype(jnp.float32)], axis=0)


def attn_kernel(n_prev, *refs):
    if n_prev:
        q_ref, k_ref, v_ref, swap_ref, cos_ref, sin_ref, k_prev_ref, v_prev_ref, ctx_ref = refs
    else:
        q_ref, k_ref, v_ref, swap_ref, cos_ref, sin_ref, ctx_ref, k_out_ref = refs
    head_dim, rows = q_ref.shape[1:]
    scale = head_dim ** -0.5 * LOG2E
    q_t = rotate(q_ref[0], swap_ref[...], cos_ref[...], sin_ref[...]).astype(jnp.bfloat16)
    k_new = rotate(k_ref[0], swap_ref[...], cos_ref[...], sin_ref[...]).T.astype(jnp.bfloat16)
    if not n_prev:
        k_out_ref[0] = k_new
    causal = lax.broadcasted_iota(jnp.int32, (Q_BLOCK, Q_BLOCK), 0) <= lax.broadcasted_iota(jnp.int32, (Q_BLOCK, Q_BLOCK), 1)
    for block in range(rows // Q_BLOCK):
        lo, hi = block * Q_BLOCK, (block + 1) * Q_BLOCK
        q_blk = q_t[:, lo:hi]
        parts = []
        if n_prev:
            parts.append((k_prev_ref[0], v_prev_ref[0]))
        if lo:
            parts.append((k_new[:lo], v_ref[0, :, :lo]))
        parts.append((k_new[lo:hi], v_ref[0, :, lo:hi]))
        scores = [jnp.dot(k_part, q_blk, preferred_element_type=jnp.float32) * scale for k_part, _ in parts]
        scores[-1] = jnp.where(causal, scores[-1], -1e30)
        top = functools.reduce(jnp.maximum, [jnp.max(s, axis=0, keepdims=True) for s in scores])
        exps = [jnp.exp2(s - top) for s in scores]
        total = functools.reduce(jnp.add, [jnp.sum(e, axis=0, keepdims=True) for e in exps])
        inv = 1.0 / total
        ctx = None
        for e, (_, v_part) in zip(exps, parts):
            term = jnp.dot(v_part, (e * inv).astype(jnp.bfloat16), preferred_element_type=jnp.float32)
            ctx = term if ctx is None else ctx + term
        ctx_ref[0, :, lo:hi] = ctx.astype(jnp.bfloat16)


def attention(qkv_t, swap, cos_t, sin_t, previous):
    n_heads, head_dim, rows = qkv_t.shape[0] // 3, qkv_t.shape[1], qkv_t.shape[2]
    n_prev = previous[0].shape[1] if previous else 0
    part = lambda which: pl.BlockSpec((1, head_dim, rows), lambda h: (3 * h + which, 0, 0))
    table = pl.BlockSpec((ROT_PAD, rows), lambda h: (0, 0))
    whole = pl.BlockSpec(swap.shape, lambda h: (0, 0))
    in_specs = [part(0), part(1), part(2), whole, table, table]
    operands = [qkv_t, qkv_t, qkv_t, swap, cos_t, sin_t]
    out_shape = [jax.ShapeDtypeStruct((n_heads, head_dim, rows), jnp.bfloat16)]
    out_specs = [pl.BlockSpec((1, head_dim, rows), lambda h: (h, 0, 0))]
    if previous:
        in_specs += [pl.BlockSpec((1, n_prev, head_dim), lambda h: (h, 0, 0)), pl.BlockSpec((1, head_dim, n_prev), lambda h: (3 * h + 2, 0, 0))]
        operands += list(previous)
    else:
        out_shape.append(jax.ShapeDtypeStruct((n_heads, rows, head_dim), jnp.bfloat16))
        out_specs.append(pl.BlockSpec((1, rows, head_dim), lambda h: (h, 0, 0)))
    pairs = n_heads * rows * (n_prev + rows)
    return pl.pallas_call(
        functools.partial(attn_kernel, n_prev),
        out_shape=out_shape,
        grid=(n_heads,),
        in_specs=in_specs,
        out_specs=out_specs,
        cost_estimate=pl.CostEstimate(flops=pairs * 1000, bytes_accessed=n_heads * rows * 128 * 12, transcendentals=pairs),
        name="attention",
    )(*operands)


def qkv_kernel(w_ref, ln_ref, bias_ref, out_ref):
    acc = lax.dot_general(w_ref[...], ln_ref[...], (((1,), (1,)), ((), ())), preferred_element_type=jnp.float32)
    out_ref[...] = (acc + bias_ref[...]).astype(jnp.bfloat16)


def qkv_projection(w_t, ln, bias_t):
    features, width = w_t.shape
    rows = ln.shape[0]
    block = features // 4
    return pl.pallas_call(
        qkv_kernel,
        out_shape=jax.ShapeDtypeStruct((features, rows), jnp.bfloat16),
        grid=(features // block,),
        in_specs=[pl.BlockSpec((block, width), lambda j: (j, 0)), pl.BlockSpec((rows, width), lambda j: (0, 0)),
                  pl.BlockSpec((block, 1), lambda j: (j, 0))],
        out_specs=pl.BlockSpec((block, rows), lambda j: (j, 0)),
        cost_estimate=pl.CostEstimate(flops=2 * features * width * rows, bytes_accessed=2 * features * width, transcendentals=0),
        name="qkv_projection",
    )(w_t, ln, bias_t)


def up_kernel(ln_ref, w_ref, bias_ref, out_ref):
    hidden = jnp.dot(ln_ref[...], w_ref[...], preferred_element_type=jnp.float32) + bias_ref[...]
    out_ref[...] = (0.5 * hidden * (1.0 + lax.erf(hidden * (0.5 ** 0.5)))).astype(jnp.bfloat16)


def up_projection(ln, w_up, bias, part):
    rows, width = ln.shape
    inner = w_up.shape[1] // 2
    block = 256
    return pl.pallas_call(
        up_kernel,
        out_shape=jax.ShapeDtypeStruct((rows, inner), jnp.bfloat16),
        grid=(inner // block,),
        in_specs=[pl.BlockSpec((rows, width), lambda j: (0, 0)), pl.BlockSpec((width, block), lambda j: (0, j + part * (inner // block))),
                  pl.BlockSpec((1, block), lambda j: (0, j + part * (inner // block)))],
        out_specs=pl.BlockSpec((rows, block), lambda j: (0, j)),
        cost_estimate=pl.CostEstimate(flops=2 * inner * width * rows, bytes_accessed=2 * inner * width, transcendentals=0),
        name="up_projection",
    )(ln, w_up, bias)


def down_kernel(low_ref, high_ref, ctx_t_ref, w_low_ref, w_high_ref, w_dense_ref, out_ref, ctx_ref):
    @pl.when(pl.program_id(0) == 0)
    def _():
        ctx_ref[...] = ctx_t_ref[...].T

    attn = jnp.dot(ctx_ref[...], w_dense_ref[...], preferred_element_type=jnp.float32)
    low = jnp.dot(low_ref[...], w_low_ref[...], preferred_element_type=jnp.float32)
    high = jnp.dot(high_ref[...], w_high_ref[...], preferred_element_type=jnp.float32)
    out_ref[...] = (attn + (low + high)).astype(jnp.bfloat16)


def down_projection(low, high, ctx_t, w_down, w_dense):
    rows, inner = low.shape
    features, width = w_dense.shape
    block = 256
    return pl.pallas_call(
        down_kernel,
        out_shape=jax.ShapeDtypeStruct((rows, width), jnp.bfloat16),
        grid=(width // block,),
        in_specs=[pl.BlockSpec((rows, inner), lambda j: (0, 0)), pl.BlockSpec((rows, inner), lambda j: (0, 0)),
                  pl.BlockSpec((features, rows), lambda j: (0, 0)), pl.BlockSpec((inner, block), lambda j: (0, j)),
                  pl.BlockSpec((inner, block), lambda j: (1, j)), pl.BlockSpec((features, block), lambda j: (0, j))],
        out_specs=pl.BlockSpec((rows, block), lambda j: (0, j)),
        scratch_shapes=[pltpu.VMEM((rows, features), jnp.bfloat16)],
        cost_estimate=pl.CostEstimate(flops=2 * (2 * inner + features) * width * rows, bytes_accessed=2 * (2 * inner + features) * width, transcendentals=0),
        name="down_projection",
    )(low, high, ctx_t, w_down, w_down, w_dense)


def unwritten(shape):
    return pl.pallas_call(
        lambda out_ref: None,
        out_shape=jax.ShapeDtypeStruct(shape, jnp.bfloat16),
        out_specs=pl.BlockSpec(memory_space=pl.ANY),
        name="unwritten",
    )()


def store_kernel(sel_ref, held_ref, *refs):
    *cand_refs, out_ref, buf_ref, in_sem, out_sem = refs
    pieces, block = buf_ref.shape[:2]
    slot = sel_ref[1]

    def read(cand_ref, piece):
        return pltpu.make_async_copy(cand_ref.at[pl.ds(piece * block, block)], buf_ref.at[piece], in_sem.at[piece])

    def write(piece):
        return pltpu.make_async_copy(buf_ref.at[piece], out_ref.at[slot, pl.ds(piece * block, block)], out_sem.at[piece])

    for index, cand_ref in enumerate(cand_refs):
        @pl.when(sel_ref[0] == index)
        def _():
            for piece in range(pieces):
                read(cand_ref, piece).start()
    for piece in range(pieces):
        read(cand_refs[0], piece).wait()
        write(piece).start()
    for piece in range(pieces):
        write(piece).wait()


def store_final(result, which, slot, candidates):
    rows, width = candidates[0].shape
    pieces = 4
    hbm = pl.BlockSpec(memory_space=pltpu.HBM)
    scalars = jnp.stack([which, slot]).astype(jnp.int32)
    return pl.pallas_call(
        store_kernel,
        out_shape=jax.ShapeDtypeStruct(result.shape, result.dtype),
        in_specs=[pl.BlockSpec(memory_space=pltpu.SMEM)] + [hbm] * (1 + len(candidates)),
        out_specs=hbm,
        scratch_shapes=[pltpu.VMEM((pieces, rows // pieces, width), result.dtype),
                        pltpu.SemaphoreType.DMA((pieces,)), pltpu.SemaphoreType.DMA((pieces,))],
        input_output_aliases={1: 0},
        cost_estimate=pl.CostEstimate(flops=rows * width * 300, bytes_accessed=rows * width * 4, transcendentals=0),
        name="store_final",
    )(scalars, result, *candidates)


def rotary_tables(seq_len, rot_dims, head_dim):
    half = rot_dims // 2
    inv_freq = 1.0 / (10000.0 ** (jnp.arange(0, rot_dims, 2).astype(jnp.float32) / rot_dims))
    angles = inv_freq[:, None] * jnp.arange(seq_len).astype(jnp.float32)[None, :]
    spare = ROT_PAD - rot_dims
    cos_t = jnp.concatenate([jnp.cos(angles), jnp.cos(angles), jnp.ones((spare, seq_len), jnp.float32)])
    sin_t = jnp.concatenate([jnp.sin(angles), jnp.sin(angles), jnp.zeros((spare, seq_len), jnp.float32)])
    row = lax.broadcasted_iota(jnp.int32, (ROT_PAD, head_dim), 0)
    col = lax.broadcasted_iota(jnp.int32, (ROT_PAD, head_dim), 1)
    minus = jnp.logical_and(row < half, col == row + half)
    plus = jnp.logical_and(jnp.logical_and(row >= half, row < rot_dims), col == row - half)
    swap = jnp.where(plus, 1.0, jnp.where(minus, -1.0, 0.0)).astype(jnp.bfloat16)
    return swap, cos_t, sin_t


def solution(mesh):
    n_stages, n_tp = mesh.shape["pp"], mesh.shape["tp"]
    in_specs = (P(), P("pp", None), P("pp", None), P("pp", None, "tp", None), P("pp", "tp", None),
                P("pp", "tp", None, None), P("pp", None), P("pp", None), P("pp", None),
                P("pp", None, "tp"), P("pp", "tp"), P("pp", "tp", None), P("pp", None))

    def device_fn(x_micro, ln1_gain, ln1_bias, w_qkv, b_qkv, w_dense, b_dense, ln2_gain, ln2_bias, w_up, b_up, w_down, b_down):
        n_micro, _, seq_len, width = x_micro.shape
        n_heads, head_dim = w_dense.shape[1:3]
        rows = seq_len // CHUNKS
        quarter = rows // n_tp
        stage, tp_id = lax.axis_index("pp"), lax.axis_index("tp")
        x_chunks = x_micro.reshape(n_micro * CHUNKS, rows, width)
        norms = [v[:1].astype(jnp.float32) for v in (ln1_gain, ln1_bias, ln2_gain, ln2_bias)]
        bias_sum = b_dense[0].astype(jnp.float32) + b_down[0].astype(jnp.float32)
        w_qkv_t = w_qkv[0].transpose(1, 2, 0).reshape(n_heads * 3 * head_dim, width)
        b_qkv_t = b_qkv[0].reshape(n_heads * 3 * head_dim, 1).astype(jnp.float32)
        w_qkv_t, b_qkv_t = lax.optimization_barrier((w_qkv_t, b_qkv_t))
        w_out = w_dense[0].reshape(n_heads * head_dim, width)
        up_bias = b_up[:1].astype(jnp.float32)
        swap, cos_t, sin_t = rotary_tables(seq_len, head_dim // 4, head_dim)
        tables = [(cos_t[:, c * rows:(c + 1) * rows], sin_t[:, c * rows:(c + 1) * rows]) for c in range(CHUNKS)]
        tables = lax.optimization_barrier(tables)
        ring = [(s, (s + 1) % n_stages) for s in range(n_stages)]

        def norms_of(chunk, slot, gathered):
            where_from = slot * CHUNKS + chunk
            ln_attn, ln_mlp = layer_norms(stage, where_from, x_chunks, gathered, *norms)
            from_x = lax.dynamic_slice(x_chunks, (where_from, tp_id * quarter, 0), (1, quarter, width))[0]
            from_ring = lax.dynamic_slice(gathered, (tp_id * quarter, 0), (quarter, width))
            return ln_attn, ln_mlp, jnp.where(stage == 0, from_x, from_ring)

        def attend(chunk, ln_attn, previous):
            qkv_t = qkv_projection(w_qkv_t, ln_attn, b_qkv_t).reshape(3 * n_heads, head_dim, rows)
            if previous is None:
                ctx_t, keys = attention(qkv_t, swap, *tables[chunk], None)
                previous = (keys, qkv_t)
            else:
                ctx_t, = attention(qkv_t, swap, *tables[chunk], previous)
            return ctx_t.reshape(n_heads * head_dim, rows), previous

        def scatter(partial):
            return lax.psum_scatter(partial, "tp", scatter_dimension=0, tiled=True)

        def pass_on(summed, kept):
            out = (kept.astype(jnp.float32) + bias_sum + summed.astype(jnp.float32)).astype(jnp.bfloat16)
            return lax.ppermute(out, "pp", ring)

        def gather(out):
            return lax.all_gather(out, "tp", axis=0, tiled=True)

        def to_second(final):
            return lax.ppermute(final, "pp", [(0, 2)]), lax.ppermute(final, "pp", [(0, 1)])

        def to_third(far):
            return lax.ppermute(far, "pp", [(2, 3)])

        def half(chunk, slot, gathered, previous, partial_before, kept_before):
            summed = scatter(partial_before)
            far, near = to_second(gathered)
            ln_attn, ln_mlp, kept = norms_of(chunk, slot, gathered)
            ctx_t, previous = attend(chunk, ln_attn, previous)
            low = up_projection(ln_mlp, w_up[0], up_bias, 0)
            summed, far, near, ctx_t, low, ln_mlp = lax.optimization_barrier((summed, far, near, ctx_t, low, ln_mlp))
            passed = pass_on(summed, kept_before)
            farthest = to_third(far)
            high = up_projection(ln_mlp, w_up[0], up_bias, 1)
            passed, high = lax.optimization_barrier((passed, high))
            gathered_before = gather(passed)
            partial = down_projection(low, high, ctx_t, w_down[0], w_out)
            gathered_before, partial, farthest = lax.optimization_barrier((gathered_before, partial, farthest))
            return gathered_before, partial, kept, previous, (gathered, near, far, farthest)

        def tick(step, carry):
            gathered_a, partial_b, kept_b, result = carry
            slot = jnp.clip(step, 0, n_micro - 1)
            done = jnp.maximum(step - n_stages, 0)
            gathered_b, partial_a, kept_a, previous, finals = half(0, slot, gathered_a, None, partial_b, kept_b)
            result = store_final(result, stage, done * CHUNKS, finals)
            next_a, partial_b, kept_b, _, finals = half(1, slot, gathered_b, previous, partial_a, kept_a)
            result = store_final(result, stage, done * CHUNKS + 1, finals)
            return next_a, partial_b, kept_b, result

        start = (x_chunks[0], x_chunks[1], x_chunks[0, :quarter], unwritten(x_chunks.shape))
        last_a, partial_b, kept_b, result = lax.fori_loop(0, n_micro + n_stages - 1, tick, start)
        summed = scatter(partial_b)
        far_a, near_a = to_second(last_a)
        summed, far_a, near_a = lax.optimization_barrier((summed, far_a, near_a))
        out = (kept_b.astype(jnp.float32) + bias_sum + summed.astype(jnp.float32)).astype(jnp.bfloat16)
        at_first = lax.ppermute(out, "pp", [(n_stages - 1, 0)])
        at_third = lax.ppermute(out, "pp", [(n_stages - 1, 2)])
        farthest_a = to_third(far_a)
        at_second = lax.ppermute(at_first, "pp", [(0, 1)])
        out = jnp.where(stage == 0, at_first, jnp.where(stage == 1, at_second, jnp.where(stage == 2, at_third, out)))
        last_b = gather(out)
        last = n_micro * CHUNKS - 1
        result = store_final(result, stage, jnp.int32(last - 1), (last_a, near_a, far_a, farthest_a))
        result = store_final(result, jnp.int32(0), jnp.int32(last), (last_b,))
        return result.reshape(x_micro.shape)

    return jax.shard_map(device_fn, mesh=mesh, in_specs=in_specs, out_specs=P(), check_vma=False)
```

time: 5010 us -> 2440 us (0.49)
  waiting for transfers between devices: 3400 us -> 527 us
  Pallas kernels: 0 us -> 1530 us
  matrix products: 1070 us -> 0 us
  other arithmetic: 313 us -> 76.2 us
  starting transfers between devices: 41.4 us -> 219 us
  local copies, waits for them, and re-layouts: 148 us -> 63 us
    psum x10 -> x0, waiting for transfers between devices: 3320 us -> none  [the longest x9 2460 us: tick(): summed = lax.psum(tp_part, 'tp')]
    pallas_call x0 -> x129, Pallas kernels: none -> 1530 us  [the longest x36 357 us: up_projection(): pl.pallas_call(up_kernel, out_shape=jax.ShapeDtypeStruct((rows, inner), j...]
    dot_general x18 -> x0, matrix products: 709 us -> none  [the longest x6 365 us: branch_sum(): jnp.einsum('bsd,df->bsf', ln_mlp, w_up, preferred_element_type=jnp.float32)]
    all_gather x0 -> x19, waiting for transfers between devices: none -> 401 us  [gather(): return lax.all_gather(out, 'tp', axis=0, tiled=True)]
    sub x6 -> x0, matrix products: 231 us -> none  [branch_sum(): jax.nn.softmax(jnp.where(causal, scores, -1e+30), axis=-1)]
    ppermute x9 -> x78, starting transfers between devices: 41 us -> 218 us  [the longest x19 102 us: to_second(): lax.ppermute(final, 'pp', [(0, 2)])]
    cond x6 -> x0, matrix products: 126 us -> none
    dynamic_update_slice x9 -> x0, other arithmetic: 125 us -> none  [tick(): lax.dynamic_update_index_in_dim(result, jnp.where(keep, out_act, current)...]
  transfers between devices with their start and end apart: 19 -> 116, of which waited for: 19 -> 41; matrix products, arithmetic and copies ran while one was open for 1% -> 3% of each run, Pallas kernels for 0% -> 61%
where the time goes in v1:
time: 2440 us; the launch traced here: 2430 us
  Pallas kernels  1530 us (63%)
  waiting for transfers between devices  527 us (22%)
  starting transfers between devices  219 us (9%)
  other arithmetic  76.2 us (3%)
  local copies, waits for them, and re-layouts  63 us (3%)
    all_gather x19, waiting for transfers between devices, gather(): return lax.all_gather(out, 'tp', axis=0, tiled=True)  401 us
    pallas_call x36, Pallas kernels, up_projection(): pl.pallas_call(up_kernel, out_shape=jax.ShapeDtypeStruct((rows, inner), j...  357 us
    pallas_call x18, Pallas kernels, down_projection(): pl.pallas_call(down_kernel, out_shape=jax.ShapeDtypeStruct((rows, width),...  351 us
    pallas_call x18, Pallas kernels, attention(): pl.pallas_call(functools.partial(attn_kernel, n_prev), out_shape=out_shap...  320 us
    pallas_call x18, Pallas kernels, qkv_projection(): pl.pallas_call(qkv_kernel, out_shape=jax.ShapeDtypeStruct((features, rows...  219 us
    pallas_call x18, Pallas kernels, layer_norms(): pl.pallas_call(ln_kernel, out_shape=[jax.ShapeDtypeStruct((rows, width),...  203 us
    ppermute x19, starting transfers between devices, to_second(): lax.ppermute(final, 'pp', [(0, 2)])  102 us
    pallas_call x20, Pallas kernels, store_final(): pl.pallas_call(store_kernel, out_shape=jax.ShapeDtypeStruct(result.shape,...  77 us
  transfers between devices with their start and end apart: 116, of which 41 were waited for; matrix products, arithmetic and copies ran while one was open for 3% of the time, Pallas kernels for 61%

profile of v1, /device:TPU:0, one launch (start us, length us, event | category | flops | bytes accessed | tf_op | source)
XLA Modules:
  0.0 2429.1 jit_solution(12380752608301482845)
XLA Ops:
  15.8 2284.3 %while.23 = (s32[]{:T(128)}, bf16[768,2560]{1,0:T(8,128)(2,1)}, bf16[768,2560]{1,0:T(8,128)(2,1)}, bf16[192,2560]{1,0:T(8,128)(2,1)S(1)}, bf16[12,768,2560]{2,1,...) while((s32[]{:T(128)}, bf16[768,2560]{1,0:T(8,128)(2,1)}, ...), condition=%wide.region_3.4_spmd.clone.clone, body=%wide.region_0.3_spmd.clone.clone.sunk | while | flops 78098612224 | bytes 323646592 | solution.py:353
  43.8 12.2 qkv_projection.16
  56.0 13.7 attention.16
  98.3 19.4 down_projection.16
  117.8 24.4 %all-gather.6.cloned.1.call-done.later_ref.refs_0_ = bf16[768,2560]{1,0:T(8,128)(2,1)} async-done(((bf16[192,2560]{1,0:T(8,128)(2,1)}), bf16[768,2560]{1,0:T(8,128)(2,1)}) %all-gather.6.cloned.1.call-update) | async-done | bytes 3932176 | tf_op jit(solution)/shard_map/while/body/eval_jaxpr/all_gather | solution.py:318
  184.1 21.9 attention.17
  232.1 19.5 down_projection.17
  251.6 16.7 all-gather.8.cloned.1.call-done
  298.3 12.2 qkv_projection.16
  310.5 13.7 attention.16
  352.7 19.4 down_projection.16
  372.1 23.5 all-gather.6.cloned.1.call-done.later_ref.refs_0_
  437.5 21.9 attention.17
  485.5 19.5 down_projection.17
  505.1 16.7 all-gather.8.cloned.1.call-done
  564.0 13.7 attention.16
  606.4 19.4 down_projection.16
  625.8 23.4 all-gather.6.cloned.1.call-done.later_ref.refs_0_
  691.0 21.9 attention.17
  739.1 19.5 down_projection.17
  758.6 16.7 all-gather.8.cloned.1.call-done
  817.6 13.7 attention.16
  859.9 19.4 down_projection.16
  879.4 23.4 all-gather.6.cloned.1.call-done.later_ref.refs_0_
  944.6 21.9 attention.17
  992.7 19.5 down_projection.17
  1012.2 16.7 all-gather.8.cloned.1.call-done
  1071.0 13.7 attention.16
  1113.2 19.4 down_projection.16
  1132.7 23.5 all-gather.6.cloned.1.call-done.later_ref.refs_0_
  1185.8 12.2 qkv_projection.17
  1198.0 21.9 attention.17
  1246.1 19.5 down_projection.17
  1265.6 16.6 all-gather.8.cloned.1.call-done
  1312.3 12.2 qkv_projection.16
  1324.5 13.7 attention.16
  1366.9 19.4 down_projection.16
  1386.3 23.4 all-gather.6.cloned.1.call-done.later_ref.refs_0_
  1451.5 21.9 attention.17
  1499.6 19.5 down_projection.17
  1519.1 16.7 all-gather.8.cloned.1.call-done
  1578.1 13.7 attention.16
  1620.4 19.4 down_projection.16
  1639.9 23.4 all-gather.6.cloned.1.call-done.later_ref.refs_0_
  1705.1 21.9 attention.17
  1753.1 19.5 down_projection.17
  1772.7 16.7 all-gather.8.cloned.1.call-done
  1819.4 12.2 qkv_projection.16
  1831.6 13.7 attention.16
  1874.0 19.4 down_projection.16
  1893.4 23.4 all-gather.6.cloned.1.call-done.later_ref.refs_0_
  1958.6 21.9 attention.17
  2006.7 19.5 down_projection.17
  2026.2 16.7 all-gather.8.cloned.1.call-done
  2085.0 13.7 attention.16
  2127.3 19.4 down_projection.16
  2146.7 23.5 all-gather.6.cloned.1.call-done.later_ref.refs_0_
  2199.9 12.2 qkv_projection.17
  2212.1 21.9 attention.17
  2260.1 19.5 down_projection.17
  2279.6 16.6 all-gather.8.cloned.1.call-done
  2309.2 38.1 %collective-permute-done.8.refs_2_ = bf16[768,2560]{1,0:T(8,128)(2,1)} collective-permute-done((bf16[768,2560]{1,0:T(8,128)(2,1)}, bf16[768,2560]{1,0:T(8,128)(2,1)}, u32[]{:S(2)}, u32[]{:S(2)}) %collective-permute-start.8) | collective-permute-done | bytes 3932192 | tf_op jit(solution)/shard_map/ppermute | solution.py:321
  2353.6 13.4 collective-permute-done.11
  2379.1 39.0 %all-gather.4.cloned.1.call-done.refs_0_ = bf16[768,2560]{1,0:T(8,128)(2,1)} async-done(((bf16[192,2560]{1,0:T(8,128)(2,1)}), bf16[768,2560]{1,0:T(8,128)(2,1)}) %all-gather.4.cloned.1.call-update) | async-done | bytes 3932176 | tf_op jit(solution)/shard_map/all_gather | solution.py:318
  (630 shorter events, 1216.5 us)
Async XLA Ops:
  15.9 63.7 %reduce-scatter.6.cloned.1.call-start = ((), (), s32[]{:S(2)}) async-start(), calls=%async_computation.5 | async-start | bytes 4915200 | tf_op jit(solution)/shard_map/while/body/eval_jaxpr/reduce_scatter | solution.py:311
  16.6 125.6 %all-gather.6.cloned.1.call-start = ((), (), s32[]{:S(2)}) async-start(), calls=%async_computation.6 | async-start | bytes 4915200 | tf_op jit(solution)/shard_map/while/body/eval_jaxpr/all_gather | solution.py:318
  20.9 58.6 %collective-permute-start = (bf16[768,2560]{1,0:T(8,128)(2,1)}, bf16[768,2560]{1,0:T(8,128)(2,1)}, u32[]{:S(2)}, u32[]{:S(2)}) collective-permute-start(bf16[768,2560]{1,0:T(8,128)(2,1)} %copy.29.later_ref.refs_0_), channel_id=1, source_target_pairs={{0,2},{4,6},{8,10},{12,14}} | collective-permute-start | bytes 11796488 | tf_op jit(solution)/shard_map/while/body/eval_jaxpr/ppermute | solution.py:321
  95.6 110.3 %reduce-scatter.8.cloned.1.call-start = ((), (), s32[]{:S(2)}) async-start(), calls=%async_computation.7 | async-start | bytes 4915200 | tf_op jit(solution)/shard_map/while/body/eval_jaxpr/reduce_scatter | solution.py:311
  142.2 126.1 %all-gather.8.cloned.1.call-start = ((), (), s32[]{:S(2)}) async-start(), calls=%async_computation.8 | async-start | bytes 4915200 | tf_op jit(solution)/shard_map/while/body/eval_jaxpr/all_gather | solution.py:318
  142.3 63.6 %collective-permute-start.4 = (bf16[768,2560]{1,0:T(8,128)(2,1)}, bf16[768,2560]{1,0:T(8,128)(2,1)}, u32[]{:S(2)}, u32[]{:S(2)}) collective-permute-start(bf16[768,2560]{1,0:T(8,128)(2,1)} %all-gather.6.cloned.1.call-done.later_ref.refs_0_), channel_id=1, source_target_pairs={{0,2},{4,6},{8,10},{12,14}} | collective-permute-start | bytes 11796488 | tf_op jit(solution)/shard_map/while/body/eval_jaxpr/ppermute | solution.py:321
  147.6 58.3 %collective-permute-start.5 = (bf16[768,2560]{1,0:T(8,128)(2,1)}, bf16[768,2560]{1,0:T(8,128)(2,1)}, u32[]{:S(2)}, u32[]{:S(2)}) collective-permute-start(bf16[768,2560]{1,0:T(8,128)(2,1)} %all-gather.6.cloned.1.call-done.later_ref.refs_0_), channel_id=1, source_target_pairs={{0,1},{4,5},{8,9},{12,13}} | collective-permute-start | bytes 11796488 | tf_op jit(solution)/shard_map/while/body/eval_jaxpr/ppermute | solution.py:321
  272.3 61.8 %reduce-scatter.6.cloned.1.call-start = ((), (), s32[]{:S(2)}) async-start(), calls=%async_computation.5 | async-start | bytes 4915200 | tf_op jit(solution)/shard_map/while/body/eval_jaxpr/reduce_scatter | solution.py:311
  272.9 122.8 %all-gather.6.cloned.1.call-start = ((), (), s32[]{:S(2)}) async-start(), calls=%async_computation.6 | async-start | bytes 4915200 | tf_op jit(solution)/shard_map/while/body/eval_jaxpr/all_gather | solution.py:318
  277.2 56.9 %collective-permute-start = (bf16[768,2560]{1,0:T(8,128)(2,1)}, bf16[768,2560]{1,0:T(8,128)(2,1)}, u32[]{:S(2)}, u32[]{:S(2)}) collective-permute-start(bf16[768,2560]{1,0:T(8,128)(2,1)} %copy.29.later_ref.refs_0_), channel_id=1, source_target_pairs={{0,2},{4,6},{8,10},{12,14}} | collective-permute-start | bytes 11796488 | tf_op jit(solution)/shard_map/while/body/eval_jaxpr/ppermute | solution.py:321
  350.1 109.3 %reduce-scatter.8.cloned.1.call-start = ((), (), s32[]{:S(2)}) async-start(), calls=%async_computation.7 | async-start | bytes 4915200 | tf_op jit(solution)/shard_map/while/body/eval_jaxpr/reduce_scatter | solution.py:311
  395.7 126.1 %all-gather.8.cloned.1.call-start = ((), (), s32[]{:S(2)}) async-start(), calls=%async_computation.8 | async-start | bytes 4915200 | tf_op jit(solution)/shard_map/while/body/eval_jaxpr/all_gather | solution.py:318
  395.7 63.6 %collective-permute-start.4 = (bf16[768,2560]{1,0:T(8,128)(2,1)}, bf16[768,2560]{1,0:T(8,128)(2,1)}, u32[]{:S(2)}, u32[]{:S(2)}) collective-permute-start(bf16[768,2560]{1,0:T(8,128)(2,1)} %all-gather.6.cloned.1.call-done.later_ref.refs_0_), channel_id=1, source_target_pairs={{0,2},{4,6},{8,10},{12,14}} | collective-permute-start | bytes 11796488 | tf_op jit(solution)/shard_map/while/body/eval_jaxpr/ppermute | solution.py:321
  401.0 58.3 %collective-permute-start.5 = (bf16[768,2560]{1,0:T(8,128)(2,1)}, bf16[768,2560]{1,0:T(8,128)(2,1)}, u32[]{:S(2)}, u32[]{:S(2)}) collective-permute-start(bf16[768,2560]{1,0:T(8,128)(2,1)} %all-gather.6.cloned.1.call-done.later_ref.refs_0_), channel_id=1, source_target_pairs={{0,1},{4,5},{8,9},{12,13}} | collective-permute-start | bytes 11796488 | tf_op jit(solution)/shard_map/while/body/eval_jaxpr/ppermute | solution.py:321
  525.7 61.9 %reduce-scatter.6.cloned.1.call-start = ((), (), s32[]{:S(2)}) async-start(), calls=%async_computation.5 | async-start | bytes 4915200 | tf_op jit(solution)/shard_map/while/body/eval_jaxpr/reduce_scatter | solution.py:311
  526.4 122.8 %all-gather.6.cloned.1.call-start = ((), (), s32[]{:S(2)}) async-start(), calls=%async_computation.6 | async-start | bytes 4915200 | tf_op jit(solution)/shard_map/while/body/eval_jaxpr/all_gather | solution.py:318
  530.7 56.9 %collective-permute-start = (bf16[768,2560]{1,0:T(8,128)(2,1)}, bf16[768,2560]{1,0:T(8,128)(2,1)}, u32[]{:S(2)}, u32[]{:S(2)}) collective-permute-start(bf16[768,2560]{1,0:T(8,128)(2,1)} %copy.29.later_ref.refs_0_), channel_id=1, source_target_pairs={{0,2},{4,6},{8,10},{12,14}} | collective-permute-start | bytes 11796488 | tf_op jit(solution)/shard_map/while/body/eval_jaxpr/ppermute | solution.py:321
  603.6 109.3 %reduce-scatter.8.cloned.1.call-start = ((), (), s32[]{:S(2)}) async-start(), calls=%async_computation.7 | async-start | bytes 4915200 | tf_op jit(solution)/shard_map/while/body/eval_jaxpr/reduce_scatter | solution.py:311
  649.2 126.1 %all-gather.8.cloned.1.call-start = ((), (), s32[]{:S(2)}) async-start(), calls=%async_computation.8 | async-start | bytes 4915200 | tf_op jit(solution)/shard_map/while/body/eval_jaxpr/all_gather | solution.py:318
  649.3 63.6 %collective-permute-start.4 = (bf16[768,2560]{1,0:T(8,128)(2,1)}, bf16[768,2560]{1,0:T(8,128)(2,1)}, u32[]{:S(2)}, u32[]{:S(2)}) collective-permute-start(bf16[768,2560]{1,0:T(8,128)(2,1)} %all-gather.6.cloned.1.call-done.later_ref.refs_0_), channel_id=1, source_target_pairs={{0,2},{4,6},{8,10},{12,14}} | collective-permute-start | bytes 11796488 | tf_op jit(solution)/shard_map/while/body/eval_jaxpr/ppermute | solution.py:321
  654.6 58.3 %collective-permute-start.5 = (bf16[768,2560]{1,0:T(8,128)(2,1)}, bf16[768,2560]{1,0:T(8,128)(2,1)}, u32[]{:S(2)}, u32[]{:S(2)}) collective-permute-start(bf16[768,2560]{1,0:T(8,128)(2,1)} %all-gather.6.cloned.1.call-done.later_ref.refs_0_), channel_id=1, source_target_pairs={{0,1},{4,5},{8,9},{12,13}} | collective-permute-start | bytes 11796488 | tf_op jit(solution)/shard_map/while/body/eval_jaxpr/ppermute | solution.py:321
  779.2 61.9 %reduce-scatter.6.cloned.1.call-start = ((), (), s32[]{:S(2)}) async-start(), calls=%async_computation.5 | async-start | bytes 4915200 | tf_op jit(solution)/shard_map/while/body/eval_jaxpr/reduce_scatter | solution.py:311
  780.0 122.8 %all-gather.6.cloned.1.call-start = ((), (), s32[]{:S(2)}) async-start(), calls=%async_computation.6 | async-start | bytes 4915200 | tf_op jit(solution)/shard_map/while/body/eval_jaxpr/all_gather | solution.py:318
  784.3 56.9 %collective-permute-start = (bf16[768,2560]{1,0:T(8,128)(2,1)}, bf16[768,2560]{1,0:T(8,128)(2,1)}, u32[]{:S(2)}, u32[]{:S(2)}) collective-permute-start(bf16[768,2560]{1,0:T(8,128)(2,1)} %copy.29.later_ref.refs_0_), channel_id=1, source_target_pairs={{0,2},{4,6},{8,10},{12,14}} | collective-permute-start | bytes 11796488 | tf_op jit(solution)/shard_map/while/body/eval_jaxpr/ppermute | solution.py:321
  857.2 109.3 %reduce-scatter.8.cloned.1.call-start = ((), (), s32[]{:S(2)}) async-start(), calls=%async_computation.7 | async-start | bytes 4915200 | tf_op jit(solution)/shard_map/while/body/eval_jaxpr/reduce_scatter | solution.py:311
  902.8 126.1 %all-gather.8.cloned.1.call-start = ((), (), s32[]{:S(2)}) async-start(), calls=%async_computation.8 | async-start | bytes 4915200 | tf_op jit(solution)/shard_map/while/body/eval_jaxpr/all_gather | solution.py:318
  902.8 63.6 %collective-permute-start.4 = (bf16[768,2560]{1,0:T(8,128)(2,1)}, bf16[768,2560]{1,0:T(8,128)(2,1)}, u32[]{:S(2)}, u32[]{:S(2)}) collective-permute-start(bf16[768,2560]{1,0:T(8,128)(2,1)} %all-gather.6.cloned.1.call-done.later_ref.refs_0_), channel_id=1, source_target_pairs={{0,2},{4,6},{8,10},{12,14}} | collective-permute-start | bytes 11796488 | tf_op jit(solution)/shard_map/while/body/eval_jaxpr/ppermute | solution.py:321
  908.1 58.3 %collective-permute-start.5 = (bf16[768,2560]{1,0:T(8,128)(2,1)}, bf16[768,2560]{1,0:T(8,128)(2,1)}, u32[]{:S(2)}, u32[]{:S(2)}) collective-permute-start(bf16[768,2560]{1,0:T(8,128)(2,1)} %all-gather.6.cloned.1.call-done.later_ref.refs_0_), channel_id=1, source_target_pairs={{0,1},{4,5},{8,9},{12,13}} | collective-permute-start | bytes 11796488 | tf_op jit(solution)/shard_map/while/body/eval_jaxpr/ppermute | solution.py:321
  1032.8 61.8 %reduce-scatter.6.cloned.1.call-start = ((), (), s32[]{:S(2)}) async-start(), calls=%async_computation.5 | async-start | bytes 4915200 | tf_op jit(solution)/shard_map/while/body/eval_jaxpr/reduce_scatter | solution.py:311
  1033.4 122.8 %all-gather.6.cloned.1.call-start = ((), (), s32[]{:S(2)}) async-start(), calls=%async_computation.6 | async-start | bytes 4915200 | tf_op jit(solution)/shard_map/while/body/eval_jaxpr/all_gather | solution.py:318
  1037.7 56.9 %collective-permute-start = (bf16[768,2560]{1,0:T(8,128)(2,1)}, bf16[768,2560]{1,0:T(8,128)(2,1)}, u32[]{:S(2)}, u32[]{:S(2)}) collective-permute-start(bf16[768,2560]{1,0:T(8,128)(2,1)} %copy.29.later_ref.refs_0_), channel_id=1, source_target_pairs={{0,2},{4,6},{8,10},{12,14}} | collective-permute-start | bytes 11796488 | tf_op jit(solution)/shard_map/while/body/eval_jaxpr/ppermute | solution.py:321
  1110.6 109.3 %reduce-scatter.8.cloned.1.call-start = ((), (), s32[]{:S(2)}) async-start(), calls=%async_computation.7 | async-start | bytes 4915200 | tf_op jit(solution)/shard_map/while/body/eval_jaxpr/reduce_scatter | solution.py:311
  1156.2 126.0 %all-gather.8.cloned.1.call-start = ((), (), s32[]{:S(2)}) async-start(), calls=%async_computation.8 | async-start | bytes 4915200 | tf_op jit(solution)/shard_map/while/body/eval_jaxpr/all_gather | solution.py:318
  1156.2 63.6 %collective-permute-start.4 = (bf16[768,2560]{1,0:T(8,128)(2,1)}, bf16[768,2560]{1,0:T(8,128)(2,1)}, u32[]{:S(2)}, u32[]{:S(2)}) collective-permute-start(bf16[768,2560]{1,0:T(8,128)(2,1)} %all-gather.6.cloned.1.call-done.later_ref.refs_0_), channel_id=1, source_target_pairs={{0,2},{4,6},{8,10},{12,14}} | collective-permute-start | bytes 11796488 | tf_op jit(solution)/shard_map/while/body/eval_jaxpr/ppermute | solution.py:321
  1161.5 58.3 %collective-permute-start.5 = (bf16[768,2560]{1,0:T(8,128)(2,1)}, bf16[768,2560]{1,0:T(8,128)(2,1)}, u32[]{:S(2)}, u32[]{:S(2)}) collective-permute-start(bf16[768,2560]{1,0:T(8,128)(2,1)} %all-gather.6.cloned.1.call-done.later_ref.refs_0_), channel_id=1, source_target_pairs={{0,1},{4,5},{8,9},{12,13}} | collective-permute-start | bytes 11796488 | tf_op jit(solution)/shard_map/while/body/eval_jaxpr/ppermute | solution.py:321
  1286.2 61.9 %reduce-scatter.6.cloned.1.call-start = ((), (), s32[]{:S(2)}) async-start(), calls=%async_computation.5 | async-start | bytes 4915200 | tf_op jit(solution)/shard_map/while/body/eval_jaxpr/reduce_scatter | solution.py:311
  1286.9 122.8 %all-gather.6.cloned.1.call-start = ((), (), s32[]{:S(2)}) async-start(), calls=%async_computation.6 | async-start | bytes 4915200 | tf_op jit(solution)/shard_map/while/body/eval_jaxpr/all_gather | solution.py:318
  1291.2 56.9 %collective-permute-start = (bf16[768,2560]{1,0:T(8,128)(2,1)}, bf16[768,2560]{1,0:T(8,128)(2,1)}, u32[]{:S(2)}, u32[]{:S(2)}) collective-permute-start(bf16[768,2560]{1,0:T(8,128)(2,1)} %copy.29.later_ref.refs_0_), channel_id=1, source_target_pairs={{0,2},{4,6},{8,10},{12,14}} | collective-permute-start | bytes 11796488 | tf_op jit(solution)/shard_map/while/body/eval_jaxpr/ppermute | solution.py:321
  1364.1 109.3 %reduce-scatter.8.cloned.1.call-start = ((), (), s32[]{:S(2)}) async-start(), calls=%async_computation.7 | async-start | bytes 4915200 | tf_op jit(solution)/shard_map/while/body/eval_jaxpr/reduce_scatter | solution.py:311
  1409.7 126.1 %all-gather.8.cloned.1.call-start = ((), (), s32[]{:S(2)}) async-start(), calls=%async_computation.8 | async-start | bytes 4915200 | tf_op jit(solution)/shard_map/while/body/eval_jaxpr/all_gather | solution.py:318
  1409.7 63.6 %collective-permute-start.4 = (bf16[768,2560]{1,0:T(8,128)(2,1)}, bf16[768,2560]{1,0:T(8,128)(2,1)}, u32[]{:S(2)}, u32[]{:S(2)}) collective-permute-start(bf16[768,2560]{1,0:T(8,128)(2,1)} %all-gather.6.cloned.1.call-done.later_ref.refs_0_), channel_id=1, source_target_pairs={{0,2},{4,6},{8,10},{12,14}} | collective-permute-start | bytes 11796488 | tf_op jit(solution)/shard_map/while/body/eval_jaxpr/ppermute | solution.py:321
  1415.0 58.3 %collective-permute-start.5 = (bf16[768,2560]{1,0:T(8,128)(2,1)}, bf16[768,2560]{1,0:T(8,128)(2,1)}, u32[]{:S(2)}, u32[]{:S(2)}) collective-permute-start(bf16[768,2560]{1,0:T(8,128)(2,1)} %all-gather.6.cloned.1.call-done.later_ref.refs_0_), channel_id=1, source_target_pairs={{0,1},{4,5},{8,9},{12,13}} | collective-permute-start | bytes 11796488 | tf_op jit(solution)/shard_map/while/body/eval_jaxpr/ppermute | solution.py:321
  1539.7 61.9 %reduce-scatter.6.cloned.1.call-start = ((), (), s32[]{:S(2)}) async-start(), calls=%async_computation.5 | async-start | bytes 4915200 | tf_op jit(solution)/shard_map/while/body/eval_jaxpr/reduce_scatter | solution.py:311
  1540.5 122.8 %all-gather.6.cloned.1.call-start = ((), (), s32[]{:S(2)}) async-start(), calls=%async_computation.6 | async-start | bytes 4915200 | tf_op jit(solution)/shard_map/while/body/eval_jaxpr/all_gather | solution.py:318
  1544.8 56.9 %collective-permute-start = (bf16[768,2560]{1,0:T(8,128)(2,1)}, bf16[768,2560]{1,0:T(8,128)(2,1)}, u32[]{:S(2)}, u32[]{:S(2)}) collective-permute-start(bf16[768,2560]{1,0:T(8,128)(2,1)} %copy.29.later_ref.refs_0_), channel_id=1, source_target_pairs={{0,2},{4,6},{8,10},{12,14}} | collective-permute-start | bytes 11796488 | tf_op jit(solution)/shard_map/while/body/eval_jaxpr/ppermute | solution.py:321
  1617.7 109.3 %reduce-scatter.8.cloned.1.call-start = ((), (), s32[]{:S(2)}) async-start(), calls=%async_computation.7 | async-start | bytes 4915200 | tf_op jit(solution)/shard_map/while/body/eval_jaxpr/reduce_scatter | solution.py:311
  1663.3 126.1 %all-gather.8.cloned.1.call-start = ((), (), s32[]{:S(2)}) async-start(), calls=%async_computation.8 | async-start | bytes 4915200 | tf_op jit(solution)/shard_map/while/body/eval_jaxpr/all_gather | solution.py:318
  1663.3 63.6 %collective-permute-start.4 = (bf16[768,2560]{1,0:T(8,128)(2,1)}, bf16[768,2560]{1,0:T(8,128)(2,1)}, u32[]{:S(2)}, u32[]{:S(2)}) collective-permute-start(bf16[768,2560]{1,0:T(8,128)(2,1)} %all-gather.6.cloned.1.call-done.later_ref.refs_0_), channel_id=1, source_target_pairs={{0,2},{4,6},{8,10},{12,14}} | collective-permute-start | bytes 11796488 | tf_op jit(solution)/shard_map/while/body/eval_jaxpr/ppermute | solution.py:321
  1668.6 58.3 %collective-permute-start.5 = (bf16[768,2560]{1,0:T(8,128)(2,1)}, bf16[768,2560]{1,0:T(8,128)(2,1)}, u32[]{:S(2)}, u32[]{:S(2)}) collective-permute-start(bf16[768,2560]{1,0:T(8,128)(2,1)} %all-gather.6.cloned.1.call-done.later_ref.refs_0_), channel_id=1, source_target_pairs={{0,1},{4,5},{8,9},{12,13}} | collective-permute-start | bytes 11796488 | tf_op jit(solution)/shard_map/while/body/eval_jaxpr/ppermute | solution.py:321
  1793.3 61.9 %reduce-scatter.6.cloned.1.call-start = ((), (), s32[]{:S(2)}) async-start(), calls=%async_computation.5 | async-start | bytes 4915200 | tf_op jit(solution)/shard_map/while/body/eval_jaxpr/reduce_scatter | solution.py:311
  1794.0 122.8 %all-gather.6.cloned.1.call-start = ((), (), s32[]{:S(2)}) async-start(), calls=%async_computation.6 | async-start | bytes 4915200 | tf_op jit(solution)/shard_map/while/body/eval_jaxpr/all_gather | solution.py:318
  1798.3 56.9 %collective-permute-start = (bf16[768,2560]{1,0:T(8,128)(2,1)}, bf16[768,2560]{1,0:T(8,128)(2,1)}, u32[]{:S(2)}, u32[]{:S(2)}) collective-permute-start(bf16[768,2560]{1,0:T(8,128)(2,1)} %copy.29.later_ref.refs_0_), channel_id=1, source_target_pairs={{0,2},{4,6},{8,10},{12,14}} | collective-permute-start | bytes 11796488 | tf_op jit(solution)/shard_map/while/body/eval_jaxpr/ppermute | solution.py:321
  1871.2 109.3 %reduce-scatter.8.cloned.1.call-start = ((), (), s32[]{:S(2)}) async-start(), calls=%async_computation.7 | async-start | bytes 4915200 | tf_op jit(solution)/shard_map/while/body/eval_jaxpr/reduce_scatter | solution.py:311
  1916.8 126.1 %all-gather.8.cloned.1.call-start = ((), (), s32[]{:S(2)}) async-start(), calls=%async_computation.8 | async-start | bytes 4915200 | tf_op jit(solution)/shard_map/while/body/eval_jaxpr/all_gather | solution.py:318
  1916.9 63.6 %collective-permute-start.4 = (bf16[768,2560]{1,0:T(8,128)(2,1)}, bf16[768,2560]{1,0:T(8,128)(2,1)}, u32[]{:S(2)}, u32[]{:S(2)}) collective-permute-start(bf16[768,2560]{1,0:T(8,128)(2,1)} %all-gather.6.cloned.1.call-done.later_ref.refs_0_), channel_id=1, source_target_pairs={{0,2},{4,6},{8,10},{12,14}} | collective-permute-start | bytes 11796488 | tf_op jit(solution)/shard_map/while/body/eval_jaxpr/ppermute | solution.py:321
  1922.2 58.3 %collective-permute-start.5 = (bf16[768,2560]{1,0:T(8,128)(2,1)}, bf16[768,2560]{1,0:T(8,128)(2,1)}, u32[]{:S(2)}, u32[]{:S(2)}) collective-permute-start(bf16[768,2560]{1,0:T(8,128)(2,1)} %all-gather.6.cloned.1.call-done.later_ref.refs_0_), channel_id=1, source_target_pairs={{0,1},{4,5},{8,9},{12,13}} | collective-permute-start | bytes 11796488 | tf_op jit(solution)/shard_map/while/body/eval_jaxpr/ppermute | solution.py:321
  2046.8 61.8 %reduce-scatter.6.cloned.1.call-start = ((), (), s32[]{:S(2)}) async-start(), calls=%async_computation.5 | async-start | bytes 4915200 | tf_op jit(solution)/shard_map/while/body/eval_jaxpr/reduce_scatter | solution.py:311
  2047.4 122.8 %all-gather.6.cloned.1.call-start = ((), (), s32[]{:S(2)}) async-start(), calls=%async_computation.6 | async-start | bytes 4915200 | tf_op jit(solution)/shard_map/while/body/eval_jaxpr/all_gather | solution.py:318
  2051.7 56.9 %collective-permute-start = (bf16[768,2560]{1,0:T(8,128)(2,1)}, bf16[768,2560]{1,0:T(8,128)(2,1)}, u32[]{:S(2)}, u32[]{:S(2)}) collective-permute-start(bf16[768,2560]{1,0:T(8,128)(2,1)} %copy.29.later_ref.refs_0_), channel_id=1, source_target_pairs={{0,2},{4,6},{8,10},{12,14}} | collective-permute-start | bytes 11796488 | tf_op jit(solution)/shard_map/while/body/eval_jaxpr/ppermute | solution.py:321
  2124.7 109.3 %reduce-scatter.8.cloned.1.call-start = ((), (), s32[]{:S(2)}) async-start(), calls=%async_computation.7 | async-start | bytes 4915200 | tf_op jit(solution)/shard_map/while/body/eval_jaxpr/reduce_scatter | solution.py:311
  2170.2 126.0 %all-gather.8.cloned.1.call-start = ((), (), s32[]{:S(2)}) async-start(), calls=%async_computation.8 | async-start | bytes 4915200 | tf_op jit(solution)/shard_map/while/body/eval_jaxpr/all_gather | solution.py:318
  2170.3 63.6 %collective-permute-start.4 = (bf16[768,2560]{1,0:T(8,128)(2,1)}, bf16[768,2560]{1,0:T(8,128)(2,1)}, u32[]{:S(2)}, u32[]{:S(2)}) collective-permute-start(bf16[768,2560]{1,0:T(8,128)(2,1)} %all-gather.6.cloned.1.call-done.later_ref.refs_0_), channel_id=1, source_target_pairs={{0,2},{4,6},{8,10},{12,14}} | collective-permute-start | bytes 11796488 | tf_op jit(solution)/shard_map/while/body/eval_jaxpr/ppermute | solution.py:321
  2175.6 58.3 %collective-permute-start.5 = (bf16[768,2560]{1,0:T(8,128)(2,1)}, bf16[768,2560]{1,0:T(8,128)(2,1)}, u32[]{:S(2)}, u32[]{:S(2)}) collective-permute-start(bf16[768,2560]{1,0:T(8,128)(2,1)} %all-gather.6.cloned.1.call-done.later_ref.refs_0_), channel_id=1, source_target_pairs={{0,1},{4,5},{8,9},{12,13}} | collective-permute-start | bytes 11796488 | tf_op jit(solution)/shard_map/while/body/eval_jaxpr/ppermute | solution.py:321
  2300.7 117.4 %all-gather.4.cloned.1.call-start = ((), (), s32[]{:S(2)}) async-start(), calls=%async_computation.4 | async-start | bytes 4915200 | tf_op jit(solution)/shard_map/all_gather | solution.py:318
  (150 other events, 3034.9 us)
Sparse Core Ops, SparseCore 0:
  19.7 49.3 reduce-scatter.5
  95.7 46.4 all-gather.5
  145.2 46.5 reduce-scatter.7
  222.8 45.4 all-gather.7
  275.8 46.5 reduce-scatter.5
  350.2 45.3 all-gather.5
  398.6 46.5 reduce-scatter.7
  476.2 45.4 all-gather.7
  529.5 46.5 reduce-scatter.5
  603.8 45.3 all-gather.5
  652.2 46.5 reduce-scatter.7
  729.8 45.4 all-gather.7
  783.1 46.5 reduce-scatter.5
  857.3 45.3 all-gather.5
  905.6 46.4 reduce-scatter.7
  983.4 45.4 all-gather.7
  1036.3 46.5 reduce-scatter.5
  1110.7 45.3 all-gather.5
  1159.2 46.5 reduce-scatter.7
  1236.8 45.3 all-gather.7
  1290.0 46.4 reduce-scatter.5
  1364.3 45.3 all-gather.5
  1412.7 46.5 reduce-scatter.7
  1490.3 45.4 all-gather.7
  1543.5 46.5 reduce-scatter.5
  1617.8 45.3 all-gather.5
  1666.1 46.4 reduce-scatter.7
  1743.8 45.4 all-gather.7
  1797.1 46.5 reduce-scatter.5
  1871.4 45.3 all-gather.5
  1919.8 46.5 reduce-scatter.7
  1997.4 45.4 all-gather.7
  2050.3 46.5 reduce-scatter.5
  2124.8 45.3 all-gather.5
  2173.2 46.5 reduce-scatter.7
  2250.8 45.3 all-gather.7
Sparse Core Ops, SparseCore 1:
  2303.6 46.3 reduce-scatter.3
  2371.6 46.4 all-gather.3

commit v2 on v1

--- a/solution.py
+++ b/solution.py
@@ -14,20 +14,24 @@
 
 
 def ln_kernel(stage_ref, first_ref, later_ref, gain1_ref, bias1_ref, gain2_ref, bias2_ref, attn_ref, mlp_ref):
-    group = 16
+    group, groups = 16, 8
+    width = attn_ref.shape[1]
 
     def run(source):
         def body(index, _):
-            span = pl.ds(pl.multiple_of(index * group, group), group)
-            x_f32 = source[span, :].astype(jnp.float32)
-            centered = x_f32 - jnp.mean(x_f32, axis=-1, keepdims=True)
-            spread = jnp.mean(centered * centered, axis=-1, keepdims=True)
-            normed = centered * lax.rsqrt(spread + 1e-5)
-            attn_ref[span, :] = (normed * gain1_ref[...] + bias1_ref[...]).astype(jnp.bfloat16)
-            mlp_ref[span, :] = (normed * gain2_ref[...] + bias2_ref[...]).astype(jnp.bfloat16)
+            spans = [pl.ds(pl.multiple_of((index * groups + g) * group, group), group) for g in range(groups)]
+            means = [jnp.sum(source[span, :].astype(jnp.float32), axis=-1, keepdims=True) / width for span in spans]
+            scales = []
+            for span, mean in zip(spans, means):
+                centered = source[span, :].astype(jnp.float32) - mean
+                scales.append(lax.rsqrt(jnp.sum(centered * centered, axis=-1, keepdims=True) / width + 1e-5))
+            for span, mean, scale in zip(spans, means, scales):
+                normed = (source[span, :].astype(jnp.float32) - mean) * scale
+                attn_ref[span, :] = (normed * gain1_ref[...] + bias1_ref[...]).astype(jnp.bfloat16)
+                mlp_ref[span, :] = (normed * gain2_ref[...] + bias2_ref[...]).astype(jnp.bfloat16)
             return 0
 
-        lax.fori_loop(0, attn_ref.shape[0] // group, body, 0, unroll=2)
+        lax.fori_loop(0, attn_ref.shape[0] // (group * groups), body, 0)
 
     @pl.when(stage_ref[0] == 0)
     def _():
@@ -288,7 +292,7 @@
         up_bias = b_up[:1].astype(jnp.float32)
         swap, cos_t, sin_t = rotary_tables(seq_len, head_dim // 4, head_dim)
         tables = [(cos_t[:, c * rows:(c + 1) * rows], sin_t[:, c * rows:(c + 1) * rows]) for c in range(CHUNKS)]
-        tables = lax.optimization_barrier(tables)
+        swap, tables = lax.optimization_barrier((swap, tables))
         ring = [(s, (s + 1) % n_stages) for s in range(n_stages)]
 
         def norms_of(chunk, slot, gathered):
@@ -317,42 +321,45 @@
         def gather(out):
             return lax.all_gather(out, "tp", axis=0, tiled=True)
 
-        def to_second(final):
-            return lax.ppermute(final, "pp", [(0, 2)]), lax.ppermute(final, "pp", [(0, 1)])
+        def to_far(final):
+            return lax.ppermute(final, "pp", [(0, 2)])
+
+        def to_near(final):
+            return lax.ppermute(final, "pp", [(0, 1)])
 
         def to_third(far):
             return lax.ppermute(far, "pp", [(2, 3)])
 
-        def half(chunk, slot, gathered, previous, partial_before, kept_before):
+        def half(chunk, slot, done, gathered, previous, partial_before, kept_before, result):
             summed = scatter(partial_before)
-            far, near = to_second(gathered)
+            far = to_far(gathered)
             ln_attn, ln_mlp, kept = norms_of(chunk, slot, gathered)
             ctx_t, previous = attend(chunk, ln_attn, previous)
+            summed, far, ctx_t, ln_mlp, kept = lax.optimization_barrier((summed, far, ctx_t, ln_mlp, kept))
+            passed = pass_on(summed, kept_before)
+            high = up_projection(ln_mlp, w_up[0], up_bias, 1)
+            passed, high, far, ln_mlp, gathered = lax.optimization_barrier((passed, high, far, ln_mlp, gathered))
+            gathered_before = gather(passed)
+            near, farthest = to_near(gathered), to_third(far)
             low = up_projection(ln_mlp, w_up[0], up_bias, 0)
-            summed, far, near, ctx_t, low, ln_mlp = lax.optimization_barrier((summed, far, near, ctx_t, low, ln_mlp))
-            passed = pass_on(summed, kept_before)
-            farthest = to_third(far)
-            high = up_projection(ln_mlp, w_up[0], up_bias, 1)
-            passed, high = lax.optimization_barrier((passed, high))
-            gathered_before = gather(passed)
+            low, near, farthest = lax.optimization_barrier((low, near, farthest))
+            result = store_final(result, stage, done * CHUNKS + chunk, (gathered, near, far, farthest))
             partial = down_projection(low, high, ctx_t, w_down[0], w_out)
-            gathered_before, partial, farthest = lax.optimization_barrier((gathered_before, partial, farthest))
-            return gathered_before, partial, kept, previous, (gathered, near, far, farthest)
+            gathered_before, partial, result = lax.optimization_barrier((gathered_before, partial, result))
+            return gathered_before, partial, kept, previous, result
 
         def tick(step, carry):
             gathered_a, partial_b, kept_b, result = carry
             slot = jnp.clip(step, 0, n_micro - 1)
             done = jnp.maximum(step - n_stages, 0)
-            gathered_b, partial_a, kept_a, previous, finals = half(0, slot, gathered_a, None, partial_b, kept_b)
-            result = store_final(result, stage, done * CHUNKS, finals)
-            next_a, partial_b, kept_b, _, finals = half(1, slot, gathered_b, previous, partial_a, kept_a)
-            result = store_final(result, stage, done * CHUNKS + 1, finals)
+            gathered_b, partial_a, kept_a, previous, result = half(0, slot, done, gathered_a, None, partial_b, kept_b, result)
+            next_a, partial_b, kept_b, _, result = half(1, slot, done, gathered_b, previous, partial_a, kept_a, result)
             return next_a, partial_b, kept_b, result
 
         start = (x_chunks[0], x_chunks[1], x_chunks[0, :quarter], unwritten(x_chunks.shape))
         last_a, partial_b, kept_b, result = lax.fori_loop(0, n_micro + n_stages - 1, tick, start)
         summed = scatter(partial_b)
-        far_a, near_a = to_second(last_a)
+        far_a, near_a = to_far(last_a), to_near(last_a)
         summed, far_a, near_a = lax.optimization_barrier((summed, far_a, near_a))
         out = (kept_b.astype(jnp.float32) + bias_sum + summed.astype(jnp.float32)).astype(jnp.bfloat16)
         at_first = lax.ppermute(out, "pp", [(n_stages - 1, 0)])

time: 2440 us -> 2190 us (0.90)
  waiting for transfers between devices: 527 us -> 339 us
  local copies, waits for them, and re-layouts: 63 us -> 25.5 us
  Pallas kernels: 1530 us -> 1500 us
    all_gather x19, waiting for transfers between devices: 401 us -> 152 us  [gather(): return lax.all_gather(out, 'tp', axis=0, tiled=True)]
    while x189 -> x91, local copies, waits for them, and re-layouts: 55.4 us -> 18.4 us
    ppermute x38, waiting for transfers between devices: 38.2 us -> 69.6 us  [the longest x19 69.6 us: to_far(): return lax.ppermute(final, 'pp', [(0, 2)])]
    pallas_call x18, Pallas kernels: 203 us -> 174 us  [layer_norms(): pl.pallas_call(ln_kernel, out_shape=[jax.ShapeDtypeStruct((rows, width),...]
    reduce_scatter x19, waiting for transfers between devices: 3.08 us -> 30.5 us  [scatter(): return lax.psum_scatter(partial, 'tp', scatter_dimension=0, tiled=True)]
  transfers between devices with their start and end apart: 116 -> 116, of which waited for: 41 -> 59; matrix products, arithmetic and copies ran while one was open for 3% -> 2% of each run, Pallas kernels for 61% -> 69%
where the time goes in v2:
time: 2190 us; the launch traced here: 2180 us
  Pallas kernels  1500 us (68%)
  waiting for transfers between devices  339 us (15%)
  starting transfers between devices  217 us (10%)
  other arithmetic  80.2 us (4%)
  local copies, waits for them, and re-layouts  25.5 us (1%)
    pallas_call x36, Pallas kernels, up_projection(): pl.pallas_call(up_kernel, out_shape=jax.ShapeDtypeStruct((rows, inner), j...  356 us
    pallas_call x18, Pallas kernels, down_projection(): pl.pallas_call(down_kernel, out_shape=jax.ShapeDtypeStruct((rows, width),...  353 us
    pallas_call x18, Pallas kernels, attention(): pl.pallas_call(functools.partial(attn_kernel, n_prev), out_shape=out_shap...  320 us
    pallas_call x18, Pallas kernels, qkv_projection(): pl.pallas_call(qkv_kernel, out_shape=jax.ShapeDtypeStruct((features, rows...  219 us
    pallas_call x18, Pallas kernels, layer_norms(): pl.pallas_call(ln_kernel, out_shape=[jax.ShapeDtypeStruct((rows, width),...  174 us
    all_gather x19, waiting for transfers between devices, gather(): return lax.all_gather(out, 'tp', axis=0, tiled=True)  152 us
    ppermute x19, starting transfers between devices, to_far(): return lax.ppermute(final, 'pp', [(0, 2)])  102 us
    pallas_call x20, Pallas kernels, store_final(): pl.pallas_call(store_kernel, out_shape=jax.ShapeDtypeStruct(result.shape,...  77.1 us
  transfers between devices with their start and end apart: 116, of which 59 were waited for; matrix products, arithmetic and copies ran while one was open for 2% of the time, Pallas kernels for 69%

profile of v2, /device:TPU:0, one launch (start us, length us, event | category | flops | bytes accessed | tf_op | source)
XLA Modules:
  0.0 2175.7 jit_solution(302826644969656974)
XLA Ops:
  15.8 2030.9 %while.21 = (s32[]{:T(128)}, bf16[768,2560]{1,0:T(8,128)(2,1)}, bf16[768,2560]{1,0:T(8,128)(2,1)}, bf16[192,2560]{1,0:T(8,128)(2,1)S(1)}, bf16[12,768,2560]{2,1,...) while((s32[]{:T(128)}, bf16[768,2560]{1,0:T(8,128)(2,1)}, ...), condition=%wide.region_3.4_spmd, body=%wide.region_0.3_spmd.sunk | while | flops 78098595840 | bytes 317832288 | solution.py:360
  35.7 12.2 qkv_projection.16
  47.8 13.6 attention.16
  70.6 9.9 up_projection.32.high_ref
  105.3 19.6 down_projection.16
  148.3 12.2 qkv_projection.17
  160.5 21.9 %attention.17 = bf16[8,80,768]{2,1,0:T(8,128)(2,1)} custom-call(bf16[24,80,768]{2,1,0:T(8,128)(2,1)} %bitcast.75, bf16[24,80,768]{2,1,0:T(8,128)(2,1)} %bitcast.76, bf16[24,80,768]{2,1,0:T(8,128)(2,1)} %bitcast.77, bf16[32,80]{1,0:T(8,128)(2,1)S(1)} %get-tuple-element.1017.refs_3_, f32[32,768]{1,0:T(8,128)S(1)} %get-tuple-element.1027.refs_4_, ...), custom_call_target="tpu_custom_call" | custom-call | flops 9437184000 | bytes 9437184 | tf_op jit(solution)/shard_map/while/body/eval_jaxpr/attention/pallas_call | solution.py:126
  218.7 19.6 down_projection.17
  262.0 12.2 qkv_projection.16
  274.2 13.6 attention.16
  295.7 9.9 up_projection.32.high_ref
  330.4 19.6 down_projection.16
  373.5 12.2 qkv_projection.17
  385.7 21.9 %attention.17 = bf16[8,80,768]{2,1,0:T(8,128)(2,1)} custom-call(bf16[24,80,768]{2,1,0:T(8,128)(2,1)} %bitcast.75, bf16[24,80,768]{2,1,0:T(8,128)(2,1)} %bitcast.76, bf16[24,80,768]{2,1,0:T(8,128)(2,1)} %bitcast.77, bf16[32,80]{1,0:T(8,128)(2,1)S(1)} %get-tuple-element.1017.refs_3_, f32[32,768]{1,0:T(8,128)S(1)} %get-tuple-element.1027.refs_4_, ...), custom_call_target="tpu_custom_call" | custom-call | flops 9437184000 | bytes 9437184 | tf_op jit(solution)/shard_map/while/body/eval_jaxpr/attention/pallas_call | solution.py:126
  443.8 19.6 down_projection.17
  487.3 12.2 qkv_projection.16
  499.5 13.6 attention.16
  521.2 9.9 up_projection.32.high_ref
  555.9 19.6 down_projection.16
  598.9 12.2 qkv_projection.17
  611.1 21.9 %attention.17 = bf16[8,80,768]{2,1,0:T(8,128)(2,1)} custom-call(bf16[24,80,768]{2,1,0:T(8,128)(2,1)} %bitcast.75, bf16[24,80,768]{2,1,0:T(8,128)(2,1)} %bitcast.76, bf16[24,80,768]{2,1,0:T(8,128)(2,1)} %bitcast.77, bf16[32,80]{1,0:T(8,128)(2,1)S(1)} %get-tuple-element.1017.refs_3_, f32[32,768]{1,0:T(8,128)S(1)} %get-tuple-element.1027.refs_4_, ...), custom_call_target="tpu_custom_call" | custom-call | flops 9437184000 | bytes 9437184 | tf_op jit(solution)/shard_map/while/body/eval_jaxpr/attention/pallas_call | solution.py:126
  669.2 19.6 down_projection.17
  712.8 12.2 qkv_projection.16
  724.9 13.6 attention.16
  746.6 9.9 up_projection.32.high_ref
  781.3 19.6 down_projection.16
  824.4 12.2 qkv_projection.17
  836.6 21.9 %attention.17 = bf16[8,80,768]{2,1,0:T(8,128)(2,1)} custom-call(bf16[24,80,768]{2,1,0:T(8,128)(2,1)} %bitcast.75, bf16[24,80,768]{2,1,0:T(8,128)(2,1)} %bitcast.76, bf16[24,80,768]{2,1,0:T(8,128)(2,1)} %bitcast.77, bf16[32,80]{1,0:T(8,128)(2,1)S(1)} %get-tuple-element.1017.refs_3_, f32[32,768]{1,0:T(8,128)S(1)} %get-tuple-element.1027.refs_4_, ...), custom_call_target="tpu_custom_call" | custom-call | flops 9437184000 | bytes 9437184 | tf_op jit(solution)/shard_map/while/body/eval_jaxpr/attention/pallas_call | solution.py:126
  894.7 19.6 down_projection.17
  938.0 12.2 qkv_projection.16
  950.2 13.6 attention.16
  971.7 9.9 up_projection.32.high_ref
  1006.4 19.6 down_projection.16
  1049.5 12.2 qkv_projection.17
  1061.7 21.9 %attention.17 = bf16[8,80,768]{2,1,0:T(8,128)(2,1)} custom-call(bf16[24,80,768]{2,1,0:T(8,128)(2,1)} %bitcast.75, bf16[24,80,768]{2,1,0:T(8,128)(2,1)} %bitcast.76, bf16[24,80,768]{2,1,0:T(8,128)(2,1)} %bitcast.77, bf16[32,80]{1,0:T(8,128)(2,1)S(1)} %get-tuple-element.1017.refs_3_, f32[32,768]{1,0:T(8,128)S(1)} %get-tuple-element.1027.refs_4_, ...), custom_call_target="tpu_custom_call" | custom-call | flops 9437184000 | bytes 9437184 | tf_op jit(solution)/shard_map/while/body/eval_jaxpr/attention/pallas_call | solution.py:126
  1119.8 19.6 down_projection.17
  1163.3 12.2 qkv_projection.16
  1175.5 13.6 attention.16
  1231.8 19.6 down_projection.16
  1274.9 12.2 qkv_projection.17
  1287.1 21.9 %attention.17 = bf16[8,80,768]{2,1,0:T(8,128)(2,1)} custom-call(bf16[24,80,768]{2,1,0:T(8,128)(2,1)} %bitcast.75, bf16[24,80,768]{2,1,0:T(8,128)(2,1)} %bitcast.76, bf16[24,80,768]{2,1,0:T(8,128)(2,1)} %bitcast.77, bf16[32,80]{1,0:T(8,128)(2,1)S(1)} %get-tuple-element.1017.refs_3_, f32[32,768]{1,0:T(8,128)S(1)} %get-tuple-element.1027.refs_4_, ...), custom_call_target="tpu_custom_call" | custom-call | flops 9437184000 | bytes 9437184 | tf_op jit(solution)/shard_map/while/body/eval_jaxpr/attention/pallas_call | solution.py:126
  1345.2 19.6 down_projection.17
  1388.7 12.2 qkv_projection.16
  1400.9 13.6 attention.16
  1457.3 19.6 down_projection.16
  1500.4 12.2 qkv_projection.17
  1512.6 21.9 %attention.17 = bf16[8,80,768]{2,1,0:T(8,128)(2,1)} custom-call(bf16[24,80,768]{2,1,0:T(8,128)(2,1)} %bitcast.75, bf16[24,80,768]{2,1,0:T(8,128)(2,1)} %bitcast.76, bf16[24,80,768]{2,1,0:T(8,128)(2,1)} %bitcast.77, bf16[32,80]{1,0:T(8,128)(2,1)S(1)} %get-tuple-element.1017.refs_3_, f32[32,768]{1,0:T(8,128)S(1)} %get-tuple-element.1027.refs_4_, ...), custom_call_target="tpu_custom_call" | custom-call | flops 9437184000 | bytes 9437184 | tf_op jit(solution)/shard_map/while/body/eval_jaxpr/attention/pallas_call | solution.py:126
  1570.7 19.6 down_projection.17
  1614.2 12.2 qkv_projection.16
  1626.4 13.6 attention.16
  1648.1 9.9 up_projection.32.high_ref
  1682.7 19.6 down_projection.16
  1725.8 12.2 qkv_projection.17
  1738.0 21.9 %attention.17 = bf16[8,80,768]{2,1,0:T(8,128)(2,1)} custom-call(bf16[24,80,768]{2,1,0:T(8,128)(2,1)} %bitcast.75, bf16[24,80,768]{2,1,0:T(8,128)(2,1)} %bitcast.76, bf16[24,80,768]{2,1,0:T(8,128)(2,1)} %bitcast.77, bf16[32,80]{1,0:T(8,128)(2,1)S(1)} %get-tuple-element.1017.refs_3_, f32[32,768]{1,0:T(8,128)S(1)} %get-tuple-element.1027.refs_4_, ...), custom_call_target="tpu_custom_call" | custom-call | flops 9437184000 | bytes 9437184 | tf_op jit(solution)/shard_map/while/body/eval_jaxpr/attention/pallas_call | solution.py:126
  1796.2 19.6 down_projection.17
  1839.5 12.2 qkv_projection.16
  1851.7 13.6 attention.16
  1907.9 19.6 down_projection.16
  1951.0 12.2 qkv_projection.17
  1963.2 21.9 %attention.17 = bf16[8,80,768]{2,1,0:T(8,128)(2,1)} custom-call(bf16[24,80,768]{2,1,0:T(8,128)(2,1)} %bitcast.75, bf16[24,80,768]{2,1,0:T(8,128)(2,1)} %bitcast.76, bf16[24,80,768]{2,1,0:T(8,128)(2,1)} %bitcast.77, bf16[32,80]{1,0:T(8,128)(2,1)S(1)} %get-tuple-element.1017.refs_3_, f32[32,768]{1,0:T(8,128)S(1)} %get-tuple-element.1027.refs_4_, ...), custom_call_target="tpu_custom_call" | custom-call | flops 9437184000 | bytes 9437184 | tf_op jit(solution)/shard_map/while/body/eval_jaxpr/attention/pallas_call | solution.py:126
  2021.3 19.6 down_projection.17
  2055.8 38.1 %collective-permute-done.8.refs_2_ = bf16[768,2560]{1,0:T(8,128)(2,1)} collective-permute-done((bf16[768,2560]{1,0:T(8,128)(2,1)}, bf16[768,2560]{1,0:T(8,128)(2,1)}, u32[]{:S(2)}, u32[]{:S(2)}) %collective-permute-start.8) | collective-permute-done | bytes 3932192 | tf_op jit(solution)/shard_map/ppermute | solution.py:325
  2100.1 13.4 collective-permute-done.11
  2125.7 39.0 %all-gather.4.cloned.1.call-done.refs_0_ = bf16[768,2560]{1,0:T(8,128)(2,1)} async-done(((bf16[192,2560]{1,0:T(8,128)(2,1)}), bf16[768,2560]{1,0:T(8,128)(2,1)}) %all-gather.4.cloned.1.call-update) | async-done | bytes 3932176 | tf_op jit(solution)/shard_map/all_gather | solution.py:322
  (532 shorter events, 1117.7 us)
Async XLA Ops:
  15.8 53.2 %reduce-scatter.6.cloned.1.call-start = ((), (), s32[]{:S(2)}) async-start(), calls=%async_computation.5 | async-start | bytes 4915200 | tf_op jit(solution)/shard_map/while/body/eval_jaxpr/reduce_scatter | solution.py:315
  16.6 115.0 %all-gather.6.cloned.1.call-start = ((), (), s32[]{:S(2)}) async-start(), calls=%async_computation.6 | async-start | bytes 4915200 | tf_op jit(solution)/shard_map/while/body/eval_jaxpr/all_gather | solution.py:322
  16.6 48.3 %collective-permute-start = (bf16[768,2560]{1,0:T(8,128)(2,1)}, bf16[768,2560]{1,0:T(8,128)(2,1)}, u32[]{:S(2)}, u32[]{:S(2)}) collective-permute-start(bf16[768,2560]{1,0:T(8,128)(2,1)} %get-tuple-element.909.later_ref.refs_0_), channel_id=1, source_target_pairs={{0,2},{4,6},{8,10},{12,14}} | collective-permute-start | bytes 11796488 | tf_op jit(solution)/shard_map/while/body/eval_jaxpr/ppermute | solution.py:325
  85.1 97.4 %reduce-scatter.8.cloned.1.call-start = ((), (), s32[]{:S(2)}) async-start(), calls=%async_computation.7 | async-start | bytes 4915200 | tf_op jit(solution)/shard_map/while/body/eval_jaxpr/reduce_scatter | solution.py:315
  131.6 112.5 %all-gather.8.cloned.1.call-start = ((), (), s32[]{:S(2)}) async-start(), calls=%async_computation.8 | async-start | bytes 4915200 | tf_op jit(solution)/shard_map/while/body/eval_jaxpr/all_gather | solution.py:322
  131.6 50.8 %collective-permute-start.4 = (bf16[768,2560]{1,0:T(8,128)(2,1)}, bf16[768,2560]{1,0:T(8,128)(2,1)}, u32[]{:S(2)}, u32[]{:S(2)}) collective-permute-start(bf16[768,2560]{1,0:T(8,128)(2,1)} %all-gather.6.cloned.1.call-done.later_ref.refs_0_), channel_id=1, source_target_pairs={{0,2},{4,6},{8,10},{12,14}} | collective-permute-start | bytes 11796488 | tf_op jit(solution)/shard_map/while/body/eval_jaxpr/ppermute | solution.py:325
  244.1 50.0 %reduce-scatter.6.cloned.1.call-start = ((), (), s32[]{:S(2)}) async-start(), calls=%async_computation.5 | async-start | bytes 4915200 | tf_op jit(solution)/shard_map/while/body/eval_jaxpr/reduce_scatter | solution.py:315
  244.7 112.0 %all-gather.6.cloned.1.call-start = ((), (), s32[]{:S(2)}) async-start(), calls=%async_computation.6 | async-start | bytes 4915200 | tf_op jit(solution)/shard_map/while/body/eval_jaxpr/all_gather | solution.py:322
  244.7 46.6 %collective-permute-start = (bf16[768,2560]{1,0:T(8,128)(2,1)}, bf16[768,2560]{1,0:T(8,128)(2,1)}, u32[]{:S(2)}, u32[]{:S(2)}) collective-permute-start(bf16[768,2560]{1,0:T(8,128)(2,1)} %get-tuple-element.909.later_ref.refs_0_), channel_id=1, source_target_pairs={{0,2},{4,6},{8,10},{12,14}} | collective-permute-start | bytes 11796488 | tf_op jit(solution)/shard_map/while/body/eval_jaxpr/ppermute | solution.py:325
  310.2 97.4 %reduce-scatter.8.cloned.1.call-start = ((), (), s32[]{:S(2)}) async-start(), calls=%async_computation.7 | async-start | bytes 4915200 | tf_op jit(solution)/shard_map/while/body/eval_jaxpr/reduce_scatter | solution.py:315
  356.7 112.5 %all-gather.8.cloned.1.call-start = ((), (), s32[]{:S(2)}) async-start(), calls=%async_computation.8 | async-start | bytes 4915200 | tf_op jit(solution)/shard_map/while/body/eval_jaxpr/all_gather | solution.py:322
  356.8 50.8 %collective-permute-start.4 = (bf16[768,2560]{1,0:T(8,128)(2,1)}, bf16[768,2560]{1,0:T(8,128)(2,1)}, u32[]{:S(2)}, u32[]{:S(2)}) collective-permute-start(bf16[768,2560]{1,0:T(8,128)(2,1)} %all-gather.6.cloned.1.call-done.later_ref.refs_0_), channel_id=1, source_target_pairs={{0,2},{4,6},{8,10},{12,14}} | collective-permute-start | bytes 11796488 | tf_op jit(solution)/shard_map/while/body/eval_jaxpr/ppermute | solution.py:325
  469.3 50.4 %reduce-scatter.6.cloned.1.call-start = ((), (), s32[]{:S(2)}) async-start(), calls=%async_computation.5 | async-start | bytes 4915200 | tf_op jit(solution)/shard_map/while/body/eval_jaxpr/reduce_scatter | solution.py:315
  470.0 112.1 %all-gather.6.cloned.1.call-start = ((), (), s32[]{:S(2)}) async-start(), calls=%async_computation.6 | async-start | bytes 4915200 | tf_op jit(solution)/shard_map/while/body/eval_jaxpr/all_gather | solution.py:322
  470.0 46.6 %collective-permute-start = (bf16[768,2560]{1,0:T(8,128)(2,1)}, bf16[768,2560]{1,0:T(8,128)(2,1)}, u32[]{:S(2)}, u32[]{:S(2)}) collective-permute-start(bf16[768,2560]{1,0:T(8,128)(2,1)} %get-tuple-element.909.later_ref.refs_0_), channel_id=1, source_target_pairs={{0,2},{4,6},{8,10},{12,14}} | collective-permute-start | bytes 11796488 | tf_op jit(solution)/shard_map/while/body/eval_jaxpr/ppermute | solution.py:325
  535.7 97.3 %reduce-scatter.8.cloned.1.call-start = ((), (), s32[]{:S(2)}) async-start(), calls=%async_computation.7 | async-start | bytes 4915200 | tf_op jit(solution)/shard_map/while/body/eval_jaxpr/reduce_scatter | solution.py:315
  535.8 16.2 collective-permute-start.2
  582.2 112.5 %all-gather.8.cloned.1.call-start = ((), (), s32[]{:S(2)}) async-start(), calls=%async_computation.8 | async-start | bytes 4915200 | tf_op jit(solution)/shard_map/while/body/eval_jaxpr/all_gather | solution.py:322
  582.2 50.8 %collective-permute-start.4 = (bf16[768,2560]{1,0:T(8,128)(2,1)}, bf16[768,2560]{1,0:T(8,128)(2,1)}, u32[]{:S(2)}, u32[]{:S(2)}) collective-permute-start(bf16[768,2560]{1,0:T(8,128)(2,1)} %all-gather.6.cloned.1.call-done.later_ref.refs_0_), channel_id=1, source_target_pairs={{0,2},{4,6},{8,10},{12,14}} | collective-permute-start | bytes 11796488 | tf_op jit(solution)/shard_map/while/body/eval_jaxpr/ppermute | solution.py:325
  694.7 50.3 %reduce-scatter.6.cloned.1.call-start = ((), (), s32[]{:S(2)}) async-start(), calls=%async_computation.5 | async-start | bytes 4915200 | tf_op jit(solution)/shard_map/while/body/eval_jaxpr/reduce_scatter | solution.py:315
  695.4 112.1 %all-gather.6.cloned.1.call-start = ((), (), s32[]{:S(2)}) async-start(), calls=%async_computation.6 | async-start | bytes 4915200 | tf_op jit(solution)/shard_map/while/body/eval_jaxpr/all_gather | solution.py:322
  695.5 46.6 %collective-permute-start = (bf16[768,2560]{1,0:T(8,128)(2,1)}, bf16[768,2560]{1,0:T(8,128)(2,1)}, u32[]{:S(2)}, u32[]{:S(2)}) collective-permute-start(bf16[768,2560]{1,0:T(8,128)(2,1)} %get-tuple-element.909.later_ref.refs_0_), channel_id=1, source_target_pairs={{0,2},{4,6},{8,10},{12,14}} | collective-permute-start | bytes 11796488 | tf_op jit(solution)/shard_map/while/body/eval_jaxpr/ppermute | solution.py:325
  761.1 97.4 %reduce-scatter.8.cloned.1.call-start = ((), (), s32[]{:S(2)}) async-start(), calls=%async_computation.7 | async-start | bytes 4915200 | tf_op jit(solution)/shard_map/while/body/eval_jaxpr/reduce_scatter | solution.py:315
  807.6 112.6 %all-gather.8.cloned.1.call-start = ((), (), s32[]{:S(2)}) async-start(), calls=%async_computation.8 | async-start | bytes 4915200 | tf_op jit(solution)/shard_map/while/body/eval_jaxpr/all_gather | solution.py:322
  807.6 50.8 %collective-permute-start.4 = (bf16[768,2560]{1,0:T(8,128)(2,1)}, bf16[768,2560]{1,0:T(8,128)(2,1)}, u32[]{:S(2)}, u32[]{:S(2)}) collective-permute-start(bf16[768,2560]{1,0:T(8,128)(2,1)} %all-gather.6.cloned.1.call-done.later_ref.refs_0_), channel_id=1, source_target_pairs={{0,2},{4,6},{8,10},{12,14}} | collective-permute-start | bytes 11796488 | tf_op jit(solution)/shard_map/while/body/eval_jaxpr/ppermute | solution.py:325
  920.1 50.0 %reduce-scatter.6.cloned.1.call-start = ((), (), s32[]{:S(2)}) async-start(), calls=%async_computation.5 | async-start | bytes 4915200 | tf_op jit(solution)/shard_map/while/body/eval_jaxpr/reduce_scatter | solution.py:315
  920.7 112.0 %all-gather.6.cloned.1.call-start = ((), (), s32[]{:S(2)}) async-start(), calls=%async_computation.6 | async-start | bytes 4915200 | tf_op jit(solution)/shard_map/while/body/eval_jaxpr/all_gather | solution.py:322
  920.8 46.6 %collective-permute-start = (bf16[768,2560]{1,0:T(8,128)(2,1)}, bf16[768,2560]{1,0:T(8,128)(2,1)}, u32[]{:S(2)}, u32[]{:S(2)}) collective-permute-start(bf16[768,2560]{1,0:T(8,128)(2,1)} %get-tuple-element.909.later_ref.refs_0_), channel_id=1, source_target_pairs={{0,2},{4,6},{8,10},{12,14}} | collective-permute-start | bytes 11796488 | tf_op jit(solution)/shard_map/while/body/eval_jaxpr/ppermute | solution.py:325
  986.2 97.4 %reduce-scatter.8.cloned.1.call-start = ((), (), s32[]{:S(2)}) async-start(), calls=%async_computation.7 | async-start | bytes 4915200 | tf_op jit(solution)/shard_map/while/body/eval_jaxpr/reduce_scatter | solution.py:315
  986.3 16.2 collective-permute-start.2
  1032.7 112.5 %all-gather.8.cloned.1.call-start = ((), (), s32[]{:S(2)}) async-start(), calls=%async_computation.8 | async-start | bytes 4915200 | tf_op jit(solution)/shard_map/while/body/eval_jaxpr/all_gather | solution.py:322
  1032.8 50.8 %collective-permute-start.4 = (bf16[768,2560]{1,0:T(8,128)(2,1)}, bf16[768,2560]{1,0:T(8,128)(2,1)}, u32[]{:S(2)}, u32[]{:S(2)}) collective-permute-start(bf16[768,2560]{1,0:T(8,128)(2,1)} %all-gather.6.cloned.1.call-done.later_ref.refs_0_), channel_id=1, source_target_pairs={{0,2},{4,6},{8,10},{12,14}} | collective-permute-start | bytes 11796488 | tf_op jit(solution)/shard_map/while/body/eval_jaxpr/ppermute | solution.py:325
  1145.3 50.3 %reduce-scatter.6.cloned.1.call-start = ((), (), s32[]{:S(2)}) async-start(), calls=%async_computation.5 | async-start | bytes 4915200 | tf_op jit(solution)/shard_map/while/body/eval_jaxpr/reduce_scatter | solution.py:315
  1146.0 112.1 %all-gather.6.cloned.1.call-start = ((), (), s32[]{:S(2)}) async-start(), calls=%async_computation.6 | async-start | bytes 4915200 | tf_op jit(solution)/shard_map/while/body/eval_jaxpr/all_gather | solution.py:322
  1146.0 46.6 %collective-permute-start = (bf16[768,2560]{1,0:T(8,128)(2,1)}, bf16[768,2560]{1,0:T(8,128)(2,1)}, u32[]{:S(2)}, u32[]{:S(2)}) collective-permute-start(bf16[768,2560]{1,0:T(8,128)(2,1)} %get-tuple-element.909.later_ref.refs_0_), channel_id=1, source_target_pairs={{0,2},{4,6},{8,10},{12,14}} | collective-permute-start | bytes 11796488 | tf_op jit(solution)/shard_map/while/body/eval_jaxpr/ppermute | solution.py:325
  1211.7 97.4 %reduce-scatter.8.cloned.1.call-start = ((), (), s32[]{:S(2)}) async-start(), calls=%async_computation.7 | async-start | bytes 4915200 | tf_op jit(solution)/shard_map/while/body/eval_jaxpr/reduce_scatter | solution.py:315
  1258.1 112.5 %all-gather.8.cloned.1.call-start = ((), (), s32[]{:S(2)}) async-start(), calls=%async_computation.8 | async-start | bytes 4915200 | tf_op jit(solution)/shard_map/while/body/eval_jaxpr/all_gather | solution.py:322
  1258.2 50.8 %collective-permute-start.4 = (bf16[768,2560]{1,0:T(8,128)(2,1)}, bf16[768,2560]{1,0:T(8,128)(2,1)}, u32[]{:S(2)}, u32[]{:S(2)}) collective-permute-start(bf16[768,2560]{1,0:T(8,128)(2,1)} %all-gather.6.cloned.1.call-done.later_ref.refs_0_), channel_id=1, source_target_pairs={{0,2},{4,6},{8,10},{12,14}} | collective-permute-start | bytes 11796488 | tf_op jit(solution)/shard_map/while/body/eval_jaxpr/ppermute | solution.py:325
  1370.7 50.3 %reduce-scatter.6.cloned.1.call-start = ((), (), s32[]{:S(2)}) async-start(), calls=%async_computation.5 | async-start | bytes 4915200 | tf_op jit(solution)/shard_map/while/body/eval_jaxpr/reduce_scatter | solution.py:315
  1371.4 112.2 %all-gather.6.cloned.1.call-start = ((), (), s32[]{:S(2)}) async-start(), calls=%async_computation.6 | async-start | bytes 4915200 | tf_op jit(solution)/shard_map/while/body/eval_jaxpr/all_gather | solution.py:322
  1371.5 46.6 %collective-permute-start = (bf16[768,2560]{1,0:T(8,128)(2,1)}, bf16[768,2560]{1,0:T(8,128)(2,1)}, u32[]{:S(2)}, u32[]{:S(2)}) collective-permute-start(bf16[768,2560]{1,0:T(8,128)(2,1)} %get-tuple-element.909.later_ref.refs_0_), channel_id=1, source_target_pairs={{0,2},{4,6},{8,10},{12,14}} | collective-permute-start | bytes 11796488 | tf_op jit(solution)/shard_map/while/body/eval_jaxpr/ppermute | solution.py:325
  1437.1 97.4 %reduce-scatter.8.cloned.1.call-start = ((), (), s32[]{:S(2)}) async-start(), calls=%async_computation.7 | async-start | bytes 4915200 | tf_op jit(solution)/shard_map/while/body/eval_jaxpr/reduce_scatter | solution.py:315
  1437.2 16.2 collective-permute-start.2
  1483.6 112.6 %all-gather.8.cloned.1.call-start = ((), (), s32[]{:S(2)}) async-start(), calls=%async_computation.8 | async-start | bytes 4915200 | tf_op jit(solution)/shard_map/while/body/eval_jaxpr/all_gather | solution.py:322
  1483.7 50.8 %collective-permute-start.4 = (bf16[768,2560]{1,0:T(8,128)(2,1)}, bf16[768,2560]{1,0:T(8,128)(2,1)}, u32[]{:S(2)}, u32[]{:S(2)}) collective-permute-start(bf16[768,2560]{1,0:T(8,128)(2,1)} %all-gather.6.cloned.1.call-done.later_ref.refs_0_), channel_id=1, source_target_pairs={{0,2},{4,6},{8,10},{12,14}} | collective-permute-start | bytes 11796488 | tf_op jit(solution)/shard_map/while/body/eval_jaxpr/ppermute | solution.py:325
  1596.2 50.3 %reduce-scatter.6.cloned.1.call-start = ((), (), s32[]{:S(2)}) async-start(), calls=%async_computation.5 | async-start | bytes 4915200 | tf_op jit(solution)/shard_map/while/body/eval_jaxpr/reduce_scatter | solution.py:315
  1596.9 112.2 %all-gather.6.cloned.1.call-start = ((), (), s32[]{:S(2)}) async-start(), calls=%async_computation.6 | async-start | bytes 4915200 | tf_op jit(solution)/shard_map/while/body/eval_jaxpr/all_gather | solution.py:322
  1596.9 46.6 %collective-permute-start = (bf16[768,2560]{1,0:T(8,128)(2,1)}, bf16[768,2560]{1,0:T(8,128)(2,1)}, u32[]{:S(2)}, u32[]{:S(2)}) collective-permute-start(bf16[768,2560]{1,0:T(8,128)(2,1)} %get-tuple-element.909.later_ref.refs_0_), channel_id=1, source_target_pairs={{0,2},{4,6},{8,10},{12,14}} | collective-permute-start | bytes 11796488 | tf_op jit(solution)/shard_map/while/body/eval_jaxpr/ppermute | solution.py:325
  1662.6 97.4 %reduce-scatter.8.cloned.1.call-start = ((), (), s32[]{:S(2)}) async-start(), calls=%async_computation.7 | async-start | bytes 4915200 | tf_op jit(solution)/shard_map/while/body/eval_jaxpr/reduce_scatter | solution.py:315
  1662.6 16.3 collective-permute-start.2
  1709.1 112.5 %all-gather.8.cloned.1.call-start = ((), (), s32[]{:S(2)}) async-start(), calls=%async_computation.8 | async-start | bytes 4915200 | tf_op jit(solution)/shard_map/while/body/eval_jaxpr/all_gather | solution.py:322
  1709.1 50.8 %collective-permute-start.4 = (bf16[768,2560]{1,0:T(8,128)(2,1)}, bf16[768,2560]{1,0:T(8,128)(2,1)}, u32[]{:S(2)}, u32[]{:S(2)}) collective-permute-start(bf16[768,2560]{1,0:T(8,128)(2,1)} %all-gather.6.cloned.1.call-done.later_ref.refs_0_), channel_id=1, source_target_pairs={{0,2},{4,6},{8,10},{12,14}} | collective-permute-start | bytes 11796488 | tf_op jit(solution)/shard_map/while/body/eval_jaxpr/ppermute | solution.py:325
  1821.6 50.0 %reduce-scatter.6.cloned.1.call-start = ((), (), s32[]{:S(2)}) async-start(), calls=%async_computation.5 | async-start | bytes 4915200 | tf_op jit(solution)/shard_map/while/body/eval_jaxpr/reduce_scatter | solution.py:315
  1822.2 112.0 %all-gather.6.cloned.1.call-start = ((), (), s32[]{:S(2)}) async-start(), calls=%async_computation.6 | async-start | bytes 4915200 | tf_op jit(solution)/shard_map/while/body/eval_jaxpr/all_gather | solution.py:322
  1822.2 46.6 %collective-permute-start = (bf16[768,2560]{1,0:T(8,128)(2,1)}, bf16[768,2560]{1,0:T(8,128)(2,1)}, u32[]{:S(2)}, u32[]{:S(2)}) collective-permute-start(bf16[768,2560]{1,0:T(8,128)(2,1)} %get-tuple-element.909.later_ref.refs_0_), channel_id=1, source_target_pairs={{0,2},{4,6},{8,10},{12,14}} | collective-permute-start | bytes 11796488 | tf_op jit(solution)/shard_map/while/body/eval_jaxpr/ppermute | solution.py:325
  1887.7 97.4 %reduce-scatter.8.cloned.1.call-start = ((), (), s32[]{:S(2)}) async-start(), calls=%async_computation.7 | async-start | bytes 4915200 | tf_op jit(solution)/shard_map/while/body/eval_jaxpr/reduce_scatter | solution.py:315
  1887.8 16.2 collective-permute-start.2
  1934.2 112.6 %all-gather.8.cloned.1.call-start = ((), (), s32[]{:S(2)}) async-start(), calls=%async_computation.8 | async-start | bytes 4915200 | tf_op jit(solution)/shard_map/while/body/eval_jaxpr/all_gather | solution.py:322
  1934.2 50.8 %collective-permute-start.4 = (bf16[768,2560]{1,0:T(8,128)(2,1)}, bf16[768,2560]{1,0:T(8,128)(2,1)}, u32[]{:S(2)}, u32[]{:S(2)}) collective-permute-start(bf16[768,2560]{1,0:T(8,128)(2,1)} %all-gather.6.cloned.1.call-done.later_ref.refs_0_), channel_id=1, source_target_pairs={{0,2},{4,6},{8,10},{12,14}} | collective-permute-start | bytes 11796488 | tf_op jit(solution)/shard_map/while/body/eval_jaxpr/ppermute | solution.py:325
  2046.7 49.9 %reduce-scatter.4.cloned.1.call-start = ((), (), s32[]{:S(2)}) async-start(), calls=%async_computation.3 | async-start | bytes 4915200 | tf_op jit(solution)/shard_map/reduce_scatter | solution.py:315
  2047.3 117.4 %all-gather.4.cloned.1.call-start = ((), (), s32[]{:S(2)}) async-start(), calls=%async_computation.4 | async-start | bytes 4915200 | tf_op jit(solution)/shard_map/all_gather | solution.py:322
  2047.4 46.6 %collective-permute-start.8 = (bf16[768,2560]{1,0:T(8,128)(2,1)}, bf16[768,2560]{1,0:T(8,128)(2,1)}, u32[]{:S(2)}, u32[]{:S(2)}) collective-permute-start(bf16[768,2560]{1,0:T(8,128)(2,1)} %get-tuple-element.612.refs_0_), channel_id=1, source_target_pairs={{0,2},{4,6},{8,10},{12,14}} | collective-permute-start | bytes 11796488 | tf_op jit(solution)/shard_map/ppermute | solution.py:325
  2052.6 41.3 %collective-permute-start.9 = (bf16[768,2560]{1,0:T(8,128)(2,1)}, bf16[768,2560]{1,0:T(8,128)(2,1)}, u32[]{:S(2)}, u32[]{:S(2)}) collective-permute-start(bf16[768,2560]{1,0:T(8,128)(2,1)} %get-tuple-element.612.refs_0_), channel_id=1, source_target_pairs={{0,1},{4,5},{8,9},{12,13}} | collective-permute-start | bytes 11796488 | tf_op jit(solution)/shard_map/ppermute | solution.py:328
  2099.4 16.4 collective-permute-start.13
  (105 other events, 1237.8 us)
Sparse Core Ops, SparseCore 0:
  19.7 49.3 reduce-scatter.5
  85.2 46.2 all-gather.5
  134.6 46.4 reduce-scatter.7
  198.7 45.3 all-gather.7
  247.6 46.4 reduce-scatter.5
  310.3 46.3 all-gather.5
  359.7 46.4 reduce-scatter.7
  423.9 45.3 all-gather.7
  473.1 46.5 reduce-scatter.5
  535.8 46.2 all-gather.5
  585.1 46.4 reduce-scatter.7
  649.3 45.3 all-gather.7
  698.5 46.4 reduce-scatter.5
  761.2 46.2 all-gather.5
  810.4 46.4 reduce-scatter.7
  874.7 45.3 all-gather.7
  923.6 46.4 reduce-scatter.5
  986.4 46.2 all-gather.5
  1035.7 46.4 reduce-scatter.7
  1099.8 45.3 all-gather.7
  1149.1 46.4 reduce-scatter.5
  1211.8 46.2 all-gather.5
  1261.1 46.4 reduce-scatter.7
  1325.3 45.3 all-gather.7
  1374.5 46.4 reduce-scatter.5
  1437.2 46.3 all-gather.5
  1486.4 46.4 reduce-scatter.7
  1550.7 45.3 all-gather.7
  1600.0 46.4 reduce-scatter.5
  1662.7 46.3 all-gather.5
  1712.1 46.4 reduce-scatter.7
  1776.2 45.3 all-gather.7
  1825.1 46.4 reduce-scatter.5
  1887.8 46.2 all-gather.5
  1937.2 46.4 reduce-scatter.7
  2001.3 45.3 all-gather.7
Sparse Core Ops, SparseCore 1:
  2050.2 46.3 reduce-scatter.3
  2118.2 46.4 all-gather.3
